TPU v7x, 32 devices: a whole 2x2x4 slice. The times are simulated.
32 devices in a mesh: blk: 16 (over z, y, core), rows: 2 (over x).
Axes of the slice: x: 2, y: 2, z: 4, core: 2. Of those that a mesh axis runs over, the one named last changes fastest.
Arguments:
- columns: float32 [2048, 1280], P('blk', 'rows'), may hold values from -9 to 9
- right_factor: float32 [2048, 512], P('blk', 'rows'), may hold values from -6 to 6
Outputs:
- new_columns: float32 [2048, 1280], P('blk', 'rows')
- new_factor: float32 [2048, 512], P('blk', 'rows')
All inputs are finite; a program needn't handle non-finite values.
Results may differ from a plain program's by a relative error of at most 0.0003.
Values sent between devices are 32-bit elements; how exact they have to be, the bound alone decides.
A program may use at most 64 MiB of HBM per device.

v0:
```python
import jax
import jax.numpy as jnp
from jax import lax
from jax.sharding import PartitionSpec as P

STEPS = 6


HIGHEST_PREC = lax.Precision.HIGHEST


def shifted(block, axis, distance):
    devices = range(lax.axis_size(axis))
    route = [((i - distance) % len(devices), i) for i in devices]
    return lax.ppermute(block, axis, route)


def orth_factor(square):
    lower_factor = jnp.linalg.cholesky(jnp.dot(square.T, square, precision=HIGHEST_PREC))
    return jax.scipy.linalg.solve_triangular(lower_factor, square.T, lower=True).T


def rotation(pair_gram):
    first_turn = orth_factor(pair_gram)
    return orth_factor(jnp.dot(pair_gram, first_turn, precision=HIGHEST_PREC))


def gram_of(upper_rows, lower_rows):
    return lax.dot_general(upper_rows, lower_rows, (((1,), (1,)), ((), ())), precision=HIGHEST_PREC)


def rotate(rotation_matrix, blocks):
    return lax.dot_general(
        rotation_matrix, blocks, (((0,), (0,)), ((), ())), precision=HIGHEST_PREC
    )


def body(columns, right_factor):
    block_width = columns.shape[0] // 2
    stay_gram, moving_gram = lax.psum(
        (
            gram_of(columns[:block_width], columns[:block_width]),
            gram_of(columns[block_width:], columns[block_width:]),
        ),
        "rows",
    )

    def advance_cross(step_index, loop_state):
        column_pair, factor_pair, stay_gram, moving_gram = loop_state
        cross_term = lax.psum(gram_of(column_pair[:block_width], column_pair[block_width:]), "rows")
        upper_half = jnp.concatenate([stay_gram, cross_term], 1)
        lower_half = jnp.concatenate([cross_term.T, moving_gram], 1)
        pair_gram = jnp.concatenate([upper_half, lower_half], 0)
        rotation_matrix = rotation(pair_gram)
        column_pair = rotate(rotation_matrix, column_pair)
        factor_pair = rotate(rotation_matrix, factor_pair)
        rotated_gram = rotate(
            rotation_matrix, jnp.dot(pair_gram, rotation_matrix, precision=HIGHEST_PREC)
        )
        arrived = shifted(
            (
                column_pair[block_width:],
                factor_pair[block_width:],
                rotated_gram[block_width:, block_width:],
            ),
            "blk",
            1,
        )
        return (
            jnp.concatenate([column_pair[:block_width], arrived[0]], 0),
            jnp.concatenate([factor_pair[:block_width], arrived[1]], 0),
            rotated_gram[:block_width, :block_width],
            arrived[2],
        )

    result = lax.fori_loop(0, STEPS, advance_cross, (columns, right_factor, stay_gram, moving_gram))
    return (result[0], result[1])


def solution(mesh):
    return jax.shard_map(
        body,
        mesh=mesh,
        in_specs=(P("blk", "rows"), P("blk", "rows")),
        out_specs=(P("blk", "rows"), P("blk", "rows")),
        check_vma=False,
    )
```

profile of v0, /device:TPU:0, one launch (start us, length us, event | category | flops | bytes accessed | tf_op | source)
XLA Modules:
  0.0 402.2 jit_solution(8088612820644958071)
XLA Ops:
  2.2 10.4 %all-reduce = (f32[64,64]{1,0:T(8,128)S(1)}, f32[64,64]{1,0:T(8,128)S(1)}) all-reduce(f32[64,64]{1,0:T(8,128)S(1)} %fusion.17, f32[64,64]{1,0:T(8,128)S(1)} %fusion.15), channel_id=1, replica_groups=mesh['blk'=16,'rows'=2] {'rows'}, use_global_device_ids=true, to_apply=%region_0.0 | all-reduce | flops 8192 | bytes 65536 | tf_op jit(solution)/shard_map/psum | solution.py:40
  12.7 388.7 %while.16 = (s32[]{:T(128)}, f32[128,640]{1,0:T(8,128)S(1)}, f32[128,256]{1,0:T(8,128)S(1)}, f32[64,64]{1,0:T(8,128)S(1)}, f32[64,64]{1,0:T(8,128)S(1)}, /*index=5*/s32[]{:T(128)}) while((s32[]{:T(128)}, f32[128,640]{1,0:T(8,128)S(1)}, f32[128,256]{1,0:T(8,128)S(1)}, f32[64,64]{1,0:T(8,128)S(1)}, f32[64,64]{1,0:T(8,128)S(1)}, ...), condition=%wide.region_6.9_spmd, body=%wide.region_2.8_spmd.sunk | while | flops 384241920 | bytes 6834369 | solution.py:76
  20.7 11.7 %cholesky.144 = f32[128,128]{1,0:T(8,128)S(1)} custom-call(f32[128,128]{1,0:T(8,128)S(1)} %fusion.103), custom_call_target="Cholesky" | custom-call | tf_op jit(solution)/shard_map/while/body/eval_jaxpr/jit(cholesky)/cholesky | solution.py:19
  33.7 9.8 %custom-call.10 = f32[1,128,128]{1,2,0:T(8,128)S(1)} custom-call(f32[1,128,128]{2,1,0:T(8,128)S(1)} %fusion.105), custom_call_target="InvertDiagBlocksLowerTriangular" | custom-call | tf_op jit(solution)/shard_map/while/body/eval_jaxpr/jit(_solve_triangular)/triangular_solve | solution.py:20
  44.5 11.7 %cholesky.145 = f32[128,128]{1,0:T(8,128)S(1)} custom-call(f32[128,128]{1,0:T(8,128)S(1)} %fusion.109), custom_call_target="Cholesky" | custom-call | tf_op jit(solution)/shard_map/while/body/eval_jaxpr/jit(cholesky)/cholesky | solution.py:19
  57.6 9.8 %custom-call.11 = f32[1,128,128]{1,2,0:T(8,128)S(1)} custom-call(f32[1,128,128]{2,1,0:T(8,128)S(1)} %fusion.110), custom_call_target="InvertDiagBlocksLowerTriangular" | custom-call | tf_op jit(solution)/shard_map/while/body/eval_jaxpr/jit(_solve_triangular)/triangular_solve | solution.py:20
  86.5 11.7 %cholesky.144 = f32[128,128]{1,0:T(8,128)S(1)} custom-call(f32[128,128]{1,0:T(8,128)S(1)} %fusion.103), custom_call_target="Cholesky" | custom-call | tf_op jit(solution)/shard_map/while/body/eval_jaxpr/jit(cholesky)/cholesky | solution.py:19
  99.5 9.8 %custom-call.10 = f32[1,128,128]{1,2,0:T(8,128)S(1)} custom-call(f32[1,128,128]{2,1,0:T(8,128)S(1)} %fusion.105), custom_call_target="InvertDiagBlocksLowerTriangular" | custom-call | tf_op jit(solution)/shard_map/while/body/eval_jaxpr/jit(_solve_triangular)/triangular_solve | solution.py:20
  110.4 11.7 %cholesky.145 = f32[128,128]{1,0:T(8,128)S(1)} custom-call(f32[128,128]{1,0:T(8,128)S(1)} %fusion.109), custom_call_target="Cholesky" | custom-call | tf_op jit(solution)/shard_map/while/body/eval_jaxpr/jit(cholesky)/cholesky | solution.py:19
  123.4 9.8 %custom-call.11 = f32[1,128,128]{1,2,0:T(8,128)S(1)} custom-call(f32[1,128,128]{2,1,0:T(8,128)S(1)} %fusion.110), custom_call_target="InvertDiagBlocksLowerTriangular" | custom-call | tf_op jit(solution)/shard_map/while/body/eval_jaxpr/jit(_solve_triangular)/triangular_solve | solution.py:20
  150.8 11.7 %cholesky.144 = f32[128,128]{1,0:T(8,128)S(1)} custom-call(f32[128,128]{1,0:T(8,128)S(1)} %fusion.103), custom_call_target="Cholesky" | custom-call | tf_op jit(solution)/shard_map/while/body/eval_jaxpr/jit(cholesky)/cholesky | solution.py:19
  163.8 9.8 %custom-call.10 = f32[1,128,128]{1,2,0:T(8,128)S(1)} custom-call(f32[1,128,128]{2,1,0:T(8,128)S(1)} %fusion.105), custom_call_target="InvertDiagBlocksLowerTriangular" | custom-call | tf_op jit(solution)/shard_map/while/body/eval_jaxpr/jit(_solve_triangular)/triangular_solve | solution.py:20
  174.6 11.7 %cholesky.145 = f32[128,128]{1,0:T(8,128)S(1)} custom-call(f32[128,128]{1,0:T(8,128)S(1)} %fusion.109), custom_call_target="Cholesky" | custom-call | tf_op jit(solution)/shard_map/while/body/eval_jaxpr/jit(cholesky)/cholesky | solution.py:19
  187.7 9.8 %custom-call.11 = f32[1,128,128]{1,2,0:T(8,128)S(1)} custom-call(f32[1,128,128]{2,1,0:T(8,128)S(1)} %fusion.110), custom_call_target="InvertDiagBlocksLowerTriangular" | custom-call | tf_op jit(solution)/shard_map/while/body/eval_jaxpr/jit(_solve_triangular)/triangular_solve | solution.py:20
  216.0 11.7 %cholesky.144 = f32[128,128]{1,0:T(8,128)S(1)} custom-call(f32[128,128]{1,0:T(8,128)S(1)} %fusion.103), custom_call_target="Cholesky" | custom-call | tf_op jit(solution)/shard_map/while/body/eval_jaxpr/jit(cholesky)/cholesky | solution.py:19
  229.1 9.8 %custom-call.10 = f32[1,128,128]{1,2,0:T(8,128)S(1)} custom-call(f32[1,128,128]{2,1,0:T(8,128)S(1)} %fusion.105), custom_call_target="InvertDiagBlocksLowerTriangular" | custom-call | tf_op jit(solution)/shard_map/while/body/eval_jaxpr/jit(_solve_triangular)/triangular_solve | solution.py:20
  239.9 11.7 %cholesky.145 = f32[128,128]{1,0:T(8,128)S(1)} custom-call(f32[128,128]{1,0:T(8,128)S(1)} %fusion.109), custom_call_target="Cholesky" | custom-call | tf_op jit(solution)/shard_map/while/body/eval_jaxpr/jit(cholesky)/cholesky | solution.py:19
  252.9 9.8 %custom-call.11 = f32[1,128,128]{1,2,0:T(8,128)S(1)} custom-call(f32[1,128,128]{2,1,0:T(8,128)S(1)} %fusion.110), custom_call_target="InvertDiagBlocksLowerTriangular" | custom-call | tf_op jit(solution)/shard_map/while/body/eval_jaxpr/jit(_solve_triangular)/triangular_solve | solution.py:20
  280.3 11.7 %cholesky.144 = f32[128,128]{1,0:T(8,128)S(1)} custom-call(f32[128,128]{1,0:T(8,128)S(1)} %fusion.103), custom_call_target="Cholesky" | custom-call | tf_op jit(solution)/shard_map/while/body/eval_jaxpr/jit(cholesky)/cholesky | solution.py:19
  293.4 9.8 %custom-call.10 = f32[1,128,128]{1,2,0:T(8,128)S(1)} custom-call(f32[1,128,128]{2,1,0:T(8,128)S(1)} %fusion.105), custom_call_target="InvertDiagBlocksLowerTriangular" | custom-call | tf_op jit(solution)/shard_map/while/body/eval_jaxpr/jit(_solve_triangular)/triangular_solve | solution.py:20
  304.2 11.7 %cholesky.145 = f32[128,128]{1,0:T(8,128)S(1)} custom-call(f32[128,128]{1,0:T(8,128)S(1)} %fusion.109), custom_call_target="Cholesky" | custom-call | tf_op jit(solution)/shard_map/while/body/eval_jaxpr/jit(cholesky)/cholesky | solution.py:19
  345.5 11.7 %cholesky.144 = f32[128,128]{1,0:T(8,128)S(1)} custom-call(f32[128,128]{1,0:T(8,128)S(1)} %fusion.103), custom_call_target="Cholesky" | custom-call | tf_op jit(solution)/shard_map/while/body/eval_jaxpr/jit(cholesky)/cholesky | solution.py:19
  358.6 9.8 %custom-call.10 = f32[1,128,128]{1,2,0:T(8,128)S(1)} custom-call(f32[1,128,128]{2,1,0:T(8,128)S(1)} %fusion.105), custom_call_target="InvertDiagBlocksLowerTriangular" | custom-call | tf_op jit(solution)/shard_map/while/body/eval_jaxpr/jit(_solve_triangular)/triangular_solve | solution.py:20
  369.4 11.7 %cholesky.145 = f32[128,128]{1,0:T(8,128)S(1)} custom-call(f32[128,128]{1,0:T(8,128)S(1)} %fusion.109), custom_call_target="Cholesky" | custom-call | tf_op jit(solution)/shard_map/while/body/eval_jaxpr/jit(cholesky)/cholesky | solution.py:19
  (227 shorter events, 151.3 us)
Async XLA Ops:
  1.9 10.8 %copy-start.2 = (f32[128,256]{1,0:T(8,128)S(1)}, f32[128,256]{1,0:T(8,128)}, u32[]{:S(2)}) copy-start(f32[128,256]{1,0:T(8,128)} %param.8) | copy-start | bytes 393220
  68.0 6.4 %collective-permute-start.1 = (f32[64,256]{1,0:T(8,128)S(1)}, f32[64,256]{1,0:T(8,128)S(1)}, u32[]{:S(2)}, u32[]{:S(2)}) collective-permute-start(f32[64,256]{1,0:T(8,128)S(1)} %get-tuple-element.91), channel_id=1, source_target_pairs={{30,0},{0,2},{2,4},{4,6},{6,8},{8,10},{10,12},{12,14},{14,16},{16,... | collective-permute-start | bytes 196616 | tf_op jit(solution)/shard_map/while/body/eval_jaxpr/ppermute | solution.py:15
  68.5 7.7 %collective-permute-start = (f32[64,640]{1,0:T(8,128)S(1)}, f32[64,640]{1,0:T(8,128)S(1)}, u32[]{:S(2)}, u32[]{:S(2)}) collective-permute-start(f32[64,640]{1,0:T(8,128)S(1)} %get-tuple-element.89), channel_id=1, source_target_pairs={{30,0},{0,2},{2,4},{4,6},{6,8},{8,10},{10,12},{12,14},{14,16},{16,... | collective-permute-start | bytes 491528 | tf_op jit(solution)/shard_map/while/body/eval_jaxpr/ppermute | solution.py:15
  71.1 6.0 %collective-permute-start.2 = (f32[64,64]{1,0:T(8,128)S(1)}, f32[64,64]{1,0:T(8,128)S(1)}, u32[]{:S(2)}, u32[]{:S(2)}) collective-permute-start(f32[64,64]{1,0:T(8,128)S(1)} %get-tuple-element.94), channel_id=1, source_target_pairs={{30,0},{0,2},{2,4},{4,6},{6,8},{8,10},{10,12},{12,14},{14,16},{16,... | collective-permute-start | bytes 49160 | tf_op jit(solution)/shard_map/while/body/eval_jaxpr/ppermute | solution.py:15
  133.8 6.4 %collective-permute-start.1 = (f32[64,256]{1,0:T(8,128)S(1)}, f32[64,256]{1,0:T(8,128)S(1)}, u32[]{:S(2)}, u32[]{:S(2)}) collective-permute-start(f32[64,256]{1,0:T(8,128)S(1)} %get-tuple-element.91), channel_id=1, source_target_pairs={{30,0},{0,2},{2,4},{4,6},{6,8},{8,10},{10,12},{12,14},{14,16},{16,... | collective-permute-start | bytes 196616 | tf_op jit(solution)/shard_map/while/body/eval_jaxpr/ppermute | solution.py:15
  134.3 7.7 %collective-permute-start = (f32[64,640]{1,0:T(8,128)S(1)}, f32[64,640]{1,0:T(8,128)S(1)}, u32[]{:S(2)}, u32[]{:S(2)}) collective-permute-start(f32[64,640]{1,0:T(8,128)S(1)} %get-tuple-element.89), channel_id=1, source_target_pairs={{30,0},{0,2},{2,4},{4,6},{6,8},{8,10},{10,12},{12,14},{14,16},{16,... | collective-permute-start | bytes 491528 | tf_op jit(solution)/shard_map/while/body/eval_jaxpr/ppermute | solution.py:15
  135.0 7.4 %collective-permute-start.2 = (f32[64,64]{1,0:T(8,128)S(1)}, f32[64,64]{1,0:T(8,128)S(1)}, u32[]{:S(2)}, u32[]{:S(2)}) collective-permute-start(f32[64,64]{1,0:T(8,128)S(1)} %get-tuple-element.94), channel_id=1, source_target_pairs={{30,0},{0,2},{2,4},{4,6},{6,8},{8,10},{10,12},{12,14},{14,16},{16,... | collective-permute-start | bytes 49160 | tf_op jit(solution)/shard_map/while/body/eval_jaxpr/ppermute | solution.py:15
  198.1 6.4 %collective-permute-start.1 = (f32[64,256]{1,0:T(8,128)S(1)}, f32[64,256]{1,0:T(8,128)S(1)}, u32[]{:S(2)}, u32[]{:S(2)}) collective-permute-start(f32[64,256]{1,0:T(8,128)S(1)} %get-tuple-element.91), channel_id=1, source_target_pairs={{30,0},{0,2},{2,4},{4,6},{6,8},{8,10},{10,12},{12,14},{14,16},{16,... | collective-permute-start | bytes 196616 | tf_op jit(solution)/shard_map/while/body/eval_jaxpr/ppermute | solution.py:15
  198.6 7.7 %collective-permute-start = (f32[64,640]{1,0:T(8,128)S(1)}, f32[64,640]{1,0:T(8,128)S(1)}, u32[]{:S(2)}, u32[]{:S(2)}) collective-permute-start(f32[64,640]{1,0:T(8,128)S(1)} %get-tuple-element.89), channel_id=1, source_target_pairs={{30,0},{0,2},{2,4},{4,6},{6,8},{8,10},{10,12},{12,14},{14,16},{16,... | collective-permute-start | bytes 491528 | tf_op jit(solution)/shard_map/while/body/eval_jaxpr/ppermute | solution.py:15
  199.2 7.4 %collective-permute-start.2 = (f32[64,64]{1,0:T(8,128)S(1)}, f32[64,64]{1,0:T(8,128)S(1)}, u32[]{:S(2)}, u32[]{:S(2)}) collective-permute-start(f32[64,64]{1,0:T(8,128)S(1)} %get-tuple-element.94), channel_id=1, source_target_pairs={{30,0},{0,2},{2,4},{4,6},{6,8},{8,10},{10,12},{12,14},{14,16},{16,... | collective-permute-start | bytes 49160 | tf_op jit(solution)/shard_map/while/body/eval_jaxpr/ppermute | solution.py:15
  263.3 6.4 %collective-permute-start.1 = (f32[64,256]{1,0:T(8,128)S(1)}, f32[64,256]{1,0:T(8,128)S(1)}, u32[]{:S(2)}, u32[]{:S(2)}) collective-permute-start(f32[64,256]{1,0:T(8,128)S(1)} %get-tuple-element.91), channel_id=1, source_target_pairs={{30,0},{0,2},{2,4},{4,6},{6,8},{8,10},{10,12},{12,14},{14,16},{16,... | collective-permute-start | bytes 196616 | tf_op jit(solution)/shard_map/while/body/eval_jaxpr/ppermute | solution.py:15
  263.8 7.7 %collective-permute-start = (f32[64,640]{1,0:T(8,128)S(1)}, f32[64,640]{1,0:T(8,128)S(1)}, u32[]{:S(2)}, u32[]{:S(2)}) collective-permute-start(f32[64,640]{1,0:T(8,128)S(1)} %get-tuple-element.89), channel_id=1, source_target_pairs={{30,0},{0,2},{2,4},{4,6},{6,8},{8,10},{10,12},{12,14},{14,16},{16,... | collective-permute-start | bytes 491528 | tf_op jit(solution)/shard_map/while/body/eval_jaxpr/ppermute | solution.py:15
  264.5 7.4 %collective-permute-start.2 = (f32[64,64]{1,0:T(8,128)S(1)}, f32[64,64]{1,0:T(8,128)S(1)}, u32[]{:S(2)}, u32[]{:S(2)}) collective-permute-start(f32[64,64]{1,0:T(8,128)S(1)} %get-tuple-element.94), channel_id=1, source_target_pairs={{30,0},{0,2},{2,4},{4,6},{6,8},{8,10},{10,12},{12,14},{14,16},{16,... | collective-permute-start | bytes 49160 | tf_op jit(solution)/shard_map/while/body/eval_jaxpr/ppermute | solution.py:15
  327.6 6.4 %collective-permute-start.1 = (f32[64,256]{1,0:T(8,128)S(1)}, f32[64,256]{1,0:T(8,128)S(1)}, u32[]{:S(2)}, u32[]{:S(2)}) collective-permute-start(f32[64,256]{1,0:T(8,128)S(1)} %get-tuple-element.91), channel_id=1, source_target_pairs={{30,0},{0,2},{2,4},{4,6},{6,8},{8,10},{10,12},{12,14},{14,16},{16,... | collective-permute-start | bytes 196616 | tf_op jit(solution)/shard_map/while/body/eval_jaxpr/ppermute | solution.py:15
  328.1 7.7 %collective-permute-start = (f32[64,640]{1,0:T(8,128)S(1)}, f32[64,640]{1,0:T(8,128)S(1)}, u32[]{:S(2)}, u32[]{:S(2)}) collective-permute-start(f32[64,640]{1,0:T(8,128)S(1)} %get-tuple-element.89), channel_id=1, source_target_pairs={{30,0},{0,2},{2,4},{4,6},{6,8},{8,10},{10,12},{12,14},{14,16},{16,... | collective-permute-start | bytes 491528 | tf_op jit(solution)/shard_map/while/body/eval_jaxpr/ppermute | solution.py:15
  328.8 7.4 %collective-permute-start.2 = (f32[64,64]{1,0:T(8,128)S(1)}, f32[64,64]{1,0:T(8,128)S(1)}, u32[]{:S(2)}, u32[]{:S(2)}) collective-permute-start(f32[64,64]{1,0:T(8,128)S(1)} %get-tuple-element.94), channel_id=1, source_target_pairs={{30,0},{0,2},{2,4},{4,6},{6,8},{8,10},{10,12},{12,14},{14,16},{16,... | collective-permute-start | bytes 49160 | tf_op jit(solution)/shard_map/while/body/eval_jaxpr/ppermute | solution.py:15
  392.8 6.4 %collective-permute-start.1 = (f32[64,256]{1,0:T(8,128)S(1)}, f32[64,256]{1,0:T(8,128)S(1)}, u32[]{:S(2)}, u32[]{:S(2)}) collective-permute-start(f32[64,256]{1,0:T(8,128)S(1)} %get-tuple-element.91), channel_id=1, source_target_pairs={{30,0},{0,2},{2,4},{4,6},{6,8},{8,10},{10,12},{12,14},{14,16},{16,... | collective-permute-start | bytes 196616 | tf_op jit(solution)/shard_map/while/body/eval_jaxpr/ppermute | solution.py:15
  393.4 7.7 %collective-permute-start = (f32[64,640]{1,0:T(8,128)S(1)}, f32[64,640]{1,0:T(8,128)S(1)}, u32[]{:S(2)}, u32[]{:S(2)}) collective-permute-start(f32[64,640]{1,0:T(8,128)S(1)} %get-tuple-element.89), channel_id=1, source_target_pairs={{30,0},{0,2},{2,4},{4,6},{6,8},{8,10},{10,12},{12,14},{14,16},{16,... | collective-permute-start | bytes 491528 | tf_op jit(solution)/shard_map/while/body/eval_jaxpr/ppermute | solution.py:15
  394.0 7.4 %collective-permute-start.2 = (f32[64,64]{1,0:T(8,128)S(1)}, f32[64,64]{1,0:T(8,128)S(1)}, u32[]{:S(2)}, u32[]{:S(2)}) collective-permute-start(f32[64,64]{1,0:T(8,128)S(1)} %get-tuple-element.94), channel_id=1, source_target_pairs={{30,0},{0,2},{2,4},{4,6},{6,8},{8,10},{10,12},{12,14},{14,16},{16,... | collective-permute-start | bytes 49160 | tf_op jit(solution)/shard_map/while/body/eval_jaxpr/ppermute | solution.py:15
  401.4 0.7 copy-start
  401.4 0.8 copy-start.1
where the time goes:
time: 403 us; the launch traced here: 402 us
  other arithmetic  275 us (68%)
  blocking collectives  57.1 us (14%)
  waiting for transfers between devices  42.6 us (11%)
  matrix products  17.9 us (4%)
  local copies, waits for them, and re-layouts  4.83 us (1%)
    another operation x36, other arithmetic, orth_factor(): jnp.linalg.cholesky(jnp.dot(square.T, square, precision=HIGHEST_PREC))  149 us
    another operation x24, other arithmetic, orth_factor(): jax.scipy.linalg.solve_triangular(lower_factor, square.T, lower=True)  126 us
    psum x6, blocking collectives, advance_cross(): lax.psum(gram_of(column_pair[:block_width], column_pair[block_width:]), '...  46.7 us
    ppermute x18, waiting for transfers between devices, shifted(): return lax.ppermute(block, axis, route)  42.6 us
    psum x1, blocking collectives, body(): lax.psum((gram_of(columns[:block_width], columns[:block_width]), gram_of(...  10.4 us
  transfers between devices with their start and end apart: 18, of which 18 were waited for; matrix products, arithmetic and copies ran while one was open for 2% of the time, Pallas kernels for 0%

commit v1 on v0

--- a/solution.py
+++ b/solution.py
@@ -15,14 +15,10 @@
     return lax.ppermute(block, axis, route)
 
 
-def orth_factor(square):
-    lower_factor = jnp.linalg.cholesky(jnp.dot(square.T, square, precision=HIGHEST_PREC))
-    return jax.scipy.linalg.solve_triangular(lower_factor, square.T, lower=True).T
-
-
 def rotation(pair_gram):
-    first_turn = orth_factor(pair_gram)
-    return orth_factor(jnp.dot(pair_gram, first_turn, precision=HIGHEST_PREC))
+    first = jnp.linalg.cholesky(jnp.dot(pair_gram, pair_gram, precision=HIGHEST_PREC))
+    second = jnp.linalg.cholesky(jnp.dot(first.T, first, precision=HIGHEST_PREC))
+    return jax.scipy.linalg.solve_triangular(second, first.T, lower=True).T
 
 
 def gram_of(upper_rows, lower_rows):

time: 403 us -> 345 us (0.86)
  other arithmetic: 275 us -> 213 us
  matrix products: 17.9 us -> 23.3 us
    another operation x60 -> x48, other arithmetic: 274 us -> 212 us  [the longest x18 74.8 us: rotation(): jnp.linalg.cholesky(jnp.dot(first.T, first, precision=HIGHEST_PREC))]
where the time goes in v1:
time: 345 us; the launch traced here: 344 us
  other arithmetic  213 us (62%)
  blocking collectives  57.1 us (17%)
  waiting for transfers between devices  42.3 us (12%)
  matrix products  23.3 us (7%)
  local copies, waits for them, and re-layouts  4.8 us (1%)
    another operation x18, other arithmetic, rotation(): jnp.linalg.cholesky(jnp.dot(first.T, first, precision=HIGHEST_PREC))  74.8 us
    another operation x18, other arithmetic, rotation(): jnp.linalg.cholesky(jnp.dot(pair_gram, pair_gram, precision=HIGHEST_PREC))  74.3 us
    another operation x12, other arithmetic, rotation(): return jax.scipy.linalg.solve_triangular(second, first.T, lower=True).T  63.1 us
    psum x6, blocking collectives, advance_cross(): lax.psum(gram_of(column_pair[:block_width], column_pair[block_width:]), '...  46.7 us
    ppermute x18, waiting for transfers between devices, shifted(): return lax.ppermute(block, axis, route)  42.3 us
    psum x1, blocking collectives, body(): lax.psum((gram_of(columns[:block_width], columns[:block_width]), gram_of(...  10.4 us
  transfers between devices with their start and end apart: 18, of which 18 were waited for; matrix products, arithmetic and copies ran while one was open for 2% of the time, Pallas kernels for 0%

profile of v1, /device:TPU:0, one launch (start us, length us, event | category | flops | bytes accessed | tf_op | source)
XLA Modules:
  0.0 344.3 jit_solution(13452265809952207676)
XLA Ops:
  2.2 10.4 %all-reduce = (f32[64,64]{1,0:T(8,128)S(1)}, f32[64,64]{1,0:T(8,128)S(1)}) all-reduce(f32[64,64]{1,0:T(8,128)S(1)} %fusion.27, f32[64,64]{1,0:T(8,128)S(1)} %fusion.25), channel_id=1, replica_groups=mesh['blk'=16,'rows'=2] {'rows'}, use_global_device_ids=true, to_apply=%region_0.0 | all-reduce | flops 8192 | bytes 65536 | tf_op jit(solution)/shard_map/psum | solution.py:36
  12.7 330.9 %while.16 = (s32[]{:T(128)}, f32[128,640]{1,0:T(8,128)S(1)}, f32[128,256]{1,0:T(8,128)S(1)}, f32[64,64]{1,0:T(8,128)S(1)}, f32[64,64]{1,0:T(8,128)S(1)}, /*index=5*/s32[]{:T(128)}) while((s32[]{:T(128)}, f32[128,640]{1,0:T(8,128)S(1)}, f32[128,256]{1,0:T(8,128)S(1)}, f32[64,64]{1,0:T(8,128)S(1)}, f32[64,64]{1,0:T(8,128)S(1)}, ...), condition=%wide.region_6.8_spmd, body=%wide.region_2.7_spmd.sunk | while | flops 333992192 | bytes 6179010 | solution.py:72
  20.7 11.7 %cholesky.175 = f32[128,128]{1,0:T(8,128)S(1)} custom-call(f32[128,128]{1,0:T(8,128)S(1)} %fusion.79), custom_call_target="Cholesky" | custom-call | tf_op jit(solution)/shard_map/while/body/eval_jaxpr/jit(cholesky)/cholesky | solution.py:19
  34.1 11.7 %cholesky.176 = f32[128,128]{1,0:T(8,128)S(1)} custom-call(f32[128,128]{1,0:T(8,128)S(1)} %fusion.82), custom_call_target="Cholesky" | custom-call | tf_op jit(solution)/shard_map/while/body/eval_jaxpr/jit(cholesky)/cholesky | solution.py:20
  47.3 9.8 %custom-call.7 = f32[1,128,128]{1,2,0:T(8,128)S(1)} custom-call(f32[1,128,128]{2,1,0:T(8,128)S(1)} %fusion.83), custom_call_target="InvertDiagBlocksLowerTriangular" | custom-call | tf_op jit(solution)/shard_map/while/body/eval_jaxpr/jit(_solve_triangular)/triangular_solve | solution.py:21
  68.0 8.3 %psum.24 = f32[64,64]{1,0:T(8,128)S(1)} all-reduce(f32[64,64]{1,0:T(8,128)S(1)} %fusion.77), channel_id=1, replica_groups=mesh['blk'=16,'rows'=2] {'rows'}, use_global_device_ids=true, to_apply=%region_3.0 | all-reduce | flops 4096 | bytes 32768 | tf_op jit(solution)/shard_map/while/body/eval_jaxpr/psum | solution.py:46
  76.9 11.7 %cholesky.175 = f32[128,128]{1,0:T(8,128)S(1)} custom-call(f32[128,128]{1,0:T(8,128)S(1)} %fusion.79), custom_call_target="Cholesky" | custom-call | tf_op jit(solution)/shard_map/while/body/eval_jaxpr/jit(cholesky)/cholesky | solution.py:19
  90.4 11.7 %cholesky.176 = f32[128,128]{1,0:T(8,128)S(1)} custom-call(f32[128,128]{1,0:T(8,128)S(1)} %fusion.82), custom_call_target="Cholesky" | custom-call | tf_op jit(solution)/shard_map/while/body/eval_jaxpr/jit(cholesky)/cholesky | solution.py:20
  103.5 9.8 %custom-call.7 = f32[1,128,128]{1,2,0:T(8,128)S(1)} custom-call(f32[1,128,128]{2,1,0:T(8,128)S(1)} %fusion.83), custom_call_target="InvertDiagBlocksLowerTriangular" | custom-call | tf_op jit(solution)/shard_map/while/body/eval_jaxpr/jit(_solve_triangular)/triangular_solve | solution.py:21
  123.6 7.4 %psum.24 = f32[64,64]{1,0:T(8,128)S(1)} all-reduce(f32[64,64]{1,0:T(8,128)S(1)} %fusion.77), channel_id=1, replica_groups=mesh['blk'=16,'rows'=2] {'rows'}, use_global_device_ids=true, to_apply=%region_3.0 | all-reduce | flops 4096 | bytes 32768 | tf_op jit(solution)/shard_map/while/body/eval_jaxpr/psum | solution.py:46
  131.6 11.7 %cholesky.175 = f32[128,128]{1,0:T(8,128)S(1)} custom-call(f32[128,128]{1,0:T(8,128)S(1)} %fusion.79), custom_call_target="Cholesky" | custom-call | tf_op jit(solution)/shard_map/while/body/eval_jaxpr/jit(cholesky)/cholesky | solution.py:19
  145.0 11.7 %cholesky.176 = f32[128,128]{1,0:T(8,128)S(1)} custom-call(f32[128,128]{1,0:T(8,128)S(1)} %fusion.82), custom_call_target="Cholesky" | custom-call | tf_op jit(solution)/shard_map/while/body/eval_jaxpr/jit(cholesky)/cholesky | solution.py:20
  158.2 9.8 %custom-call.7 = f32[1,128,128]{1,2,0:T(8,128)S(1)} custom-call(f32[1,128,128]{2,1,0:T(8,128)S(1)} %fusion.83), custom_call_target="InvertDiagBlocksLowerTriangular" | custom-call | tf_op jit(solution)/shard_map/while/body/eval_jaxpr/jit(_solve_triangular)/triangular_solve | solution.py:21
  178.2 8.3 %psum.24 = f32[64,64]{1,0:T(8,128)S(1)} all-reduce(f32[64,64]{1,0:T(8,128)S(1)} %fusion.77), channel_id=1, replica_groups=mesh['blk'=16,'rows'=2] {'rows'}, use_global_device_ids=true, to_apply=%region_3.0 | all-reduce | flops 4096 | bytes 32768 | tf_op jit(solution)/shard_map/while/body/eval_jaxpr/psum | solution.py:46
  187.1 11.7 %cholesky.175 = f32[128,128]{1,0:T(8,128)S(1)} custom-call(f32[128,128]{1,0:T(8,128)S(1)} %fusion.79), custom_call_target="Cholesky" | custom-call | tf_op jit(solution)/shard_map/while/body/eval_jaxpr/jit(cholesky)/cholesky | solution.py:19
  200.6 11.7 %cholesky.176 = f32[128,128]{1,0:T(8,128)S(1)} custom-call(f32[128,128]{1,0:T(8,128)S(1)} %fusion.82), custom_call_target="Cholesky" | custom-call | tf_op jit(solution)/shard_map/while/body/eval_jaxpr/jit(cholesky)/cholesky | solution.py:20
  213.8 9.8 %custom-call.7 = f32[1,128,128]{1,2,0:T(8,128)S(1)} custom-call(f32[1,128,128]{2,1,0:T(8,128)S(1)} %fusion.83), custom_call_target="InvertDiagBlocksLowerTriangular" | custom-call | tf_op jit(solution)/shard_map/while/body/eval_jaxpr/jit(_solve_triangular)/triangular_solve | solution.py:21
  241.8 11.7 %cholesky.175 = f32[128,128]{1,0:T(8,128)S(1)} custom-call(f32[128,128]{1,0:T(8,128)S(1)} %fusion.79), custom_call_target="Cholesky" | custom-call | tf_op jit(solution)/shard_map/while/body/eval_jaxpr/jit(cholesky)/cholesky | solution.py:19
  255.2 11.7 %cholesky.176 = f32[128,128]{1,0:T(8,128)S(1)} custom-call(f32[128,128]{1,0:T(8,128)S(1)} %fusion.82), custom_call_target="Cholesky" | custom-call | tf_op jit(solution)/shard_map/while/body/eval_jaxpr/jit(cholesky)/cholesky | solution.py:20
  268.4 9.8 %custom-call.7 = f32[1,128,128]{1,2,0:T(8,128)S(1)} custom-call(f32[1,128,128]{2,1,0:T(8,128)S(1)} %fusion.83), custom_call_target="InvertDiagBlocksLowerTriangular" | custom-call | tf_op jit(solution)/shard_map/while/body/eval_jaxpr/jit(_solve_triangular)/triangular_solve | solution.py:21
  288.5 8.3 %psum.24 = f32[64,64]{1,0:T(8,128)S(1)} all-reduce(f32[64,64]{1,0:T(8,128)S(1)} %fusion.77), channel_id=1, replica_groups=mesh['blk'=16,'rows'=2] {'rows'}, use_global_device_ids=true, to_apply=%region_3.0 | all-reduce | flops 4096 | bytes 32768 | tf_op jit(solution)/shard_map/while/body/eval_jaxpr/psum | solution.py:46
  297.4 11.7 %cholesky.175 = f32[128,128]{1,0:T(8,128)S(1)} custom-call(f32[128,128]{1,0:T(8,128)S(1)} %fusion.79), custom_call_target="Cholesky" | custom-call | tf_op jit(solution)/shard_map/while/body/eval_jaxpr/jit(cholesky)/cholesky | solution.py:19
  310.8 11.7 %cholesky.176 = f32[128,128]{1,0:T(8,128)S(1)} custom-call(f32[128,128]{1,0:T(8,128)S(1)} %fusion.82), custom_call_target="Cholesky" | custom-call | tf_op jit(solution)/shard_map/while/body/eval_jaxpr/jit(cholesky)/cholesky | solution.py:20
  324.0 9.8 %custom-call.7 = f32[1,128,128]{1,2,0:T(8,128)S(1)} custom-call(f32[1,128,128]{2,1,0:T(8,128)S(1)} %fusion.83), custom_call_target="InvertDiagBlocksLowerTriangular" | custom-call | tf_op jit(solution)/shard_map/while/body/eval_jaxpr/jit(_solve_triangular)/triangular_solve | solution.py:21
  (197 shorter events, 100.5 us)
Async XLA Ops:
  1.9 10.8 %copy-start.2 = (f32[128,256]{1,0:T(8,128)S(1)}, f32[128,256]{1,0:T(8,128)}, u32[]{:S(2)}) copy-start(f32[128,256]{1,0:T(8,128)} %param.6) | copy-start | bytes 393220
  58.3 6.4 %collective-permute-start.1 = (f32[64,256]{1,0:T(8,128)S(1)}, f32[64,256]{1,0:T(8,128)S(1)}, u32[]{:S(2)}, u32[]{:S(2)}) collective-permute-start(f32[64,256]{1,0:T(8,128)S(1)} %get-tuple-element.90), channel_id=1, source_target_pairs={{30,0},{0,2},{2,4},{4,6},{6,8},{8,10},{10,12},{12,14},{14,16},{16,... | collective-permute-start | bytes 196616 | tf_op jit(solution)/shard_map/while/body/eval_jaxpr/ppermute | solution.py:15
  58.8 7.7 %collective-permute-start = (f32[64,640]{1,0:T(8,128)S(1)}, f32[64,640]{1,0:T(8,128)S(1)}, u32[]{:S(2)}, u32[]{:S(2)}) collective-permute-start(f32[64,640]{1,0:T(8,128)S(1)} %get-tuple-element.88), channel_id=1, source_target_pairs={{30,0},{0,2},{2,4},{4,6},{6,8},{8,10},{10,12},{12,14},{14,16},{16,... | collective-permute-start | bytes 491528 | tf_op jit(solution)/shard_map/while/body/eval_jaxpr/ppermute | solution.py:15
  61.5 6.0 %collective-permute-start.2 = (f32[64,64]{1,0:T(8,128)S(1)}, f32[64,64]{1,0:T(8,128)S(1)}, u32[]{:S(2)}, u32[]{:S(2)}) collective-permute-start(f32[64,64]{1,0:T(8,128)S(1)} %get-tuple-element.93), channel_id=1, source_target_pairs={{30,0},{0,2},{2,4},{4,6},{6,8},{8,10},{10,12},{12,14},{14,16},{16,... | collective-permute-start | bytes 49160 | tf_op jit(solution)/shard_map/while/body/eval_jaxpr/ppermute | solution.py:15
  114.6 6.4 %collective-permute-start.1 = (f32[64,256]{1,0:T(8,128)S(1)}, f32[64,256]{1,0:T(8,128)S(1)}, u32[]{:S(2)}, u32[]{:S(2)}) collective-permute-start(f32[64,256]{1,0:T(8,128)S(1)} %get-tuple-element.90), channel_id=1, source_target_pairs={{30,0},{0,2},{2,4},{4,6},{6,8},{8,10},{10,12},{12,14},{14,16},{16,... | collective-permute-start | bytes 196616 | tf_op jit(solution)/shard_map/while/body/eval_jaxpr/ppermute | solution.py:15
  115.1 7.7 %collective-permute-start = (f32[64,640]{1,0:T(8,128)S(1)}, f32[64,640]{1,0:T(8,128)S(1)}, u32[]{:S(2)}, u32[]{:S(2)}) collective-permute-start(f32[64,640]{1,0:T(8,128)S(1)} %get-tuple-element.88), channel_id=1, source_target_pairs={{30,0},{0,2},{2,4},{4,6},{6,8},{8,10},{10,12},{12,14},{14,16},{16,... | collective-permute-start | bytes 491528 | tf_op jit(solution)/shard_map/while/body/eval_jaxpr/ppermute | solution.py:15
  115.8 7.3 %collective-permute-start.2 = (f32[64,64]{1,0:T(8,128)S(1)}, f32[64,64]{1,0:T(8,128)S(1)}, u32[]{:S(2)}, u32[]{:S(2)}) collective-permute-start(f32[64,64]{1,0:T(8,128)S(1)} %get-tuple-element.93), channel_id=1, source_target_pairs={{30,0},{0,2},{2,4},{4,6},{6,8},{8,10},{10,12},{12,14},{14,16},{16,... | collective-permute-start | bytes 49160 | tf_op jit(solution)/shard_map/while/body/eval_jaxpr/ppermute | solution.py:15
  169.2 6.4 %collective-permute-start.1 = (f32[64,256]{1,0:T(8,128)S(1)}, f32[64,256]{1,0:T(8,128)S(1)}, u32[]{:S(2)}, u32[]{:S(2)}) collective-permute-start(f32[64,256]{1,0:T(8,128)S(1)} %get-tuple-element.90), channel_id=1, source_target_pairs={{30,0},{0,2},{2,4},{4,6},{6,8},{8,10},{10,12},{12,14},{14,16},{16,... | collective-permute-start | bytes 196616 | tf_op jit(solution)/shard_map/while/body/eval_jaxpr/ppermute | solution.py:15
  169.7 7.7 %collective-permute-start = (f32[64,640]{1,0:T(8,128)S(1)}, f32[64,640]{1,0:T(8,128)S(1)}, u32[]{:S(2)}, u32[]{:S(2)}) collective-permute-start(f32[64,640]{1,0:T(8,128)S(1)} %get-tuple-element.88), channel_id=1, source_target_pairs={{30,0},{0,2},{2,4},{4,6},{6,8},{8,10},{10,12},{12,14},{14,16},{16,... | collective-permute-start | bytes 491528 | tf_op jit(solution)/shard_map/while/body/eval_jaxpr/ppermute | solution.py:15
  170.4 7.3 %collective-permute-start.2 = (f32[64,64]{1,0:T(8,128)S(1)}, f32[64,64]{1,0:T(8,128)S(1)}, u32[]{:S(2)}, u32[]{:S(2)}) collective-permute-start(f32[64,64]{1,0:T(8,128)S(1)} %get-tuple-element.93), channel_id=1, source_target_pairs={{30,0},{0,2},{2,4},{4,6},{6,8},{8,10},{10,12},{12,14},{14,16},{16,... | collective-permute-start | bytes 49160 | tf_op jit(solution)/shard_map/while/body/eval_jaxpr/ppermute | solution.py:15
  224.8 6.4 %collective-permute-start.1 = (f32[64,256]{1,0:T(8,128)S(1)}, f32[64,256]{1,0:T(8,128)S(1)}, u32[]{:S(2)}, u32[]{:S(2)}) collective-permute-start(f32[64,256]{1,0:T(8,128)S(1)} %get-tuple-element.90), channel_id=1, source_target_pairs={{30,0},{0,2},{2,4},{4,6},{6,8},{8,10},{10,12},{12,14},{14,16},{16,... | collective-permute-start | bytes 196616 | tf_op jit(solution)/shard_map/while/body/eval_jaxpr/ppermute | solution.py:15
  225.3 7.7 %collective-permute-start = (f32[64,640]{1,0:T(8,128)S(1)}, f32[64,640]{1,0:T(8,128)S(1)}, u32[]{:S(2)}, u32[]{:S(2)}) collective-permute-start(f32[64,640]{1,0:T(8,128)S(1)} %get-tuple-element.88), channel_id=1, source_target_pairs={{30,0},{0,2},{2,4},{4,6},{6,8},{8,10},{10,12},{12,14},{14,16},{16,... | collective-permute-start | bytes 491528 | tf_op jit(solution)/shard_map/while/body/eval_jaxpr/ppermute | solution.py:15
  226.0 7.3 %collective-permute-start.2 = (f32[64,64]{1,0:T(8,128)S(1)}, f32[64,64]{1,0:T(8,128)S(1)}, u32[]{:S(2)}, u32[]{:S(2)}) collective-permute-start(f32[64,64]{1,0:T(8,128)S(1)} %get-tuple-element.93), channel_id=1, source_target_pairs={{30,0},{0,2},{2,4},{4,6},{6,8},{8,10},{10,12},{12,14},{14,16},{16,... | collective-permute-start | bytes 49160 | tf_op jit(solution)/shard_map/while/body/eval_jaxpr/ppermute | solution.py:15
  279.4 6.4 %collective-permute-start.1 = (f32[64,256]{1,0:T(8,128)S(1)}, f32[64,256]{1,0:T(8,128)S(1)}, u32[]{:S(2)}, u32[]{:S(2)}) collective-permute-start(f32[64,256]{1,0:T(8,128)S(1)} %get-tuple-element.90), channel_id=1, source_target_pairs={{30,0},{0,2},{2,4},{4,6},{6,8},{8,10},{10,12},{12,14},{14,16},{16,... | collective-permute-start | bytes 196616 | tf_op jit(solution)/shard_map/while/body/eval_jaxpr/ppermute | solution.py:15
  280.0 7.7 %collective-permute-start = (f32[64,640]{1,0:T(8,128)S(1)}, f32[64,640]{1,0:T(8,128)S(1)}, u32[]{:S(2)}, u32[]{:S(2)}) collective-permute-start(f32[64,640]{1,0:T(8,128)S(1)} %get-tuple-element.88), channel_id=1, source_target_pairs={{30,0},{0,2},{2,4},{4,6},{6,8},{8,10},{10,12},{12,14},{14,16},{16,... | collective-permute-start | bytes 491528 | tf_op jit(solution)/shard_map/while/body/eval_jaxpr/ppermute | solution.py:15
  280.7 7.3 %collective-permute-start.2 = (f32[64,64]{1,0:T(8,128)S(1)}, f32[64,64]{1,0:T(8,128)S(1)}, u32[]{:S(2)}, u32[]{:S(2)}) collective-permute-start(f32[64,64]{1,0:T(8,128)S(1)} %get-tuple-element.93), channel_id=1, source_target_pairs={{30,0},{0,2},{2,4},{4,6},{6,8},{8,10},{10,12},{12,14},{14,16},{16,... | collective-permute-start | bytes 49160 | tf_op jit(solution)/shard_map/while/body/eval_jaxpr/ppermute | solution.py:15
  335.0 6.4 %collective-permute-start.1 = (f32[64,256]{1,0:T(8,128)S(1)}, f32[64,256]{1,0:T(8,128)S(1)}, u32[]{:S(2)}, u32[]{:S(2)}) collective-permute-start(f32[64,256]{1,0:T(8,128)S(1)} %get-tuple-element.90), channel_id=1, source_target_pairs={{30,0},{0,2},{2,4},{4,6},{6,8},{8,10},{10,12},{12,14},{14,16},{16,... | collective-permute-start | bytes 196616 | tf_op jit(solution)/shard_map/while/body/eval_jaxpr/ppermute | solution.py:15
  335.6 7.7 %collective-permute-start = (f32[64,640]{1,0:T(8,128)S(1)}, f32[64,640]{1,0:T(8,128)S(1)}, u32[]{:S(2)}, u32[]{:S(2)}) collective-permute-start(f32[64,640]{1,0:T(8,128)S(1)} %get-tuple-element.88), channel_id=1, source_target_pairs={{30,0},{0,2},{2,4},{4,6},{6,8},{8,10},{10,12},{12,14},{14,16},{16,... | collective-permute-start | bytes 491528 | tf_op jit(solution)/shard_map/while/body/eval_jaxpr/ppermute | solution.py:15
  336.3 7.3 %collective-permute-start.2 = (f32[64,64]{1,0:T(8,128)S(1)}, f32[64,64]{1,0:T(8,128)S(1)}, u32[]{:S(2)}, u32[]{:S(2)}) collective-permute-start(f32[64,64]{1,0:T(8,128)S(1)} %get-tuple-element.93), channel_id=1, source_target_pairs={{30,0},{0,2},{2,4},{4,6},{6,8},{8,10},{10,12},{12,14},{14,16},{16,... | collective-permute-start | bytes 49160 | tf_op jit(solution)/shard_map/while/body/eval_jaxpr/ppermute | solution.py:15
  343.6 0.7 copy-start
  343.6 0.8 copy-start.1

commit v2 on v1

v2 whole, which is shorter than its diff:
```python
import functools

import jax
import jax.numpy as jnp
from jax import lax
from jax.experimental import pallas as pl
from jax.experimental.pallas import tpu as pltpu
from jax.sharding import PartitionSpec as P

STEPS = 6
PANEL = 16

HIGHEST_PREC = lax.Precision.HIGHEST


def dot_nn(a, b):
    return lax.dot_general(
        a, b, (((1,), (0,)), ((), ())), precision=HIGHEST_PREC, preferred_element_type=jnp.float32
    )


def dot_nt(a, b):
    return lax.dot_general(
        a, b, (((1,), (1,)), ((), ())), precision=HIGHEST_PREC, preferred_element_type=jnp.float32
    )


def dot_tn(a, b):
    return lax.dot_general(
        a, b, (((0,), (0,)), ((), ())), precision=HIGHEST_PREC, preferred_element_type=jnp.float32
    )


def eliminate(work):
    order, width = work.shape
    panels = order // PANEL
    for panel in range(panels):
        low = panel * PANEL
        high = low + PANEL
        end = min(high + PANEL, order)
        rows = work[low:high, :]
        below = work[high:end, :] if end > high else None
        spread = [
            jnp.broadcast_to(rows[:, low + k : low + k + 1], (PANEL, 128)) for k in range(PANEL)
        ]
        spread_below = None
        if below is not None:
            spread_below = [
                jnp.broadcast_to(below[:, low + k : low + k + 1], (end - high, 128))
                for k in range(PANEL)
            ]
        done = []
        for j in range(PANEL):
            scale = lax.rsqrt(spread[j][j : j + 1, :])
            column = spread[j] * scale
            wide = jnp.concatenate([scale] * (width // 128), axis=1)
            pivot_row = rows[j : j + 1, :] * wide
            done.append(pivot_row)
            wide_column = jnp.concatenate([column] * (width // 128), axis=1)
            if j + 1 < PANEL:
                rows = rows - wide_column * pivot_row
            if below is not None:
                column_below = spread_below[j] * scale
                wide_below = jnp.concatenate([column_below] * (width // 128), axis=1)
                below = below - wide_below * pivot_row
            for k in range(j + 1, PANEL):
                head = spread[k][j : j + 1, :] * scale
                spread[k] = spread[k] - column * head
                if below is not None:
                    spread_below[k] = spread_below[k] - column_below * head
        finished = jnp.concatenate(done, axis=0)
        work[low:high, :] = finished
        if below is not None:
            work[high:end, :] = below
        if end < order:
            work[end:, :] = work[end:, :] - dot_tn(finished[:, end:order], finished)


def step_kernel(
    stay_cols, stay_fac, moving, stay_gram, cross, peer_cross, out_stay, out_fac, out_moving, out_gram,
    gram, work, solve,
):
    half, col_width = stay_cols.shape
    order = 2 * half
    fac_width = stay_fac.shape[1]
    gram_at = col_width + fac_width
    cross_term = cross[...] + peer_cross[...]
    gram[:half, :half] = stay_gram[...]
    gram[:half, half:] = cross_term
    gram[half:, :half] = cross_term.T
    gram[half:, half:] = moving[:, gram_at + half : gram_at + order]
    g = gram[...]
    work[...] = dot_nn(g, g)
    eliminate(work)
    upper = work[...]
    keep = lax.broadcasted_iota(jnp.int32, upper.shape, 0) <= lax.broadcasted_iota(
        jnp.int32, upper.shape, 1
    )
    upper = jnp.where(keep, upper, 0.0)
    solve[:, :order] = dot_nt(upper, upper)
    solve[:, order:] = upper
    eliminate(solve)
    turn = solve[:, order:]
    top, low = turn[:half], turn[half:]
    columns = jnp.concatenate([stay_cols[...], moving[:, :col_width]], axis=0)
    out_moving[:, :col_width] = dot_nn(low, columns)
    factors = jnp.concatenate([stay_fac[...], moving[:, col_width:gram_at]], axis=0)
    out_moving[:, col_width:gram_at] = dot_nn(low, factors)
    new_gram = dot_nt(dot_nn(turn, g), turn)
    out_moving[:, gram_at:] = new_gram[half:]
    out_gram[...] = new_gram[:half, :half]
    out_stay[...] = dot_nn(top, columns)
    out_fac[...] = dot_nn(top, factors)


def one_step(*operands):
    stay_cols, stay_fac, moving, stay_gram, cross, peer_cross = operands
    order = 2 * stay_cols.shape[0]
    shapes = [stay_cols, stay_fac, moving, stay_gram]
    return pl.pallas_call(
        step_kernel,
        out_shape=[jax.ShapeDtypeStruct(a.shape, a.dtype) for a in shapes],
        in_specs=[pl.BlockSpec(memory_space=pltpu.VMEM)] * 6,
        out_specs=[pl.BlockSpec(memory_space=pltpu.VMEM)] * 4,
        scratch_shapes=[
            pltpu.VMEM((order, order), jnp.float32),
            pltpu.VMEM((order, order), jnp.float32),
            pltpu.VMEM((order, 2 * order), jnp.float32),
        ],
        name="turn",
    )(*operands)


def summands(part):
    if lax.axis_size("rows") == 2:
        return part, lax.ppermute(part, "rows", [(0, 1), (1, 0)])
    return lax.psum(part, "rows"), jnp.zeros_like(part)


def gram_of(upper_rows, lower_rows):
    return dot_nt(upper_rows, lower_rows)


def body(columns, right_factor):
    half = columns.shape[0] // 2
    col_width = columns.shape[1]
    ring = lax.axis_size("blk")
    route = [((i - 1) % ring, i) for i in range(ring)]
    stay_gram, moving_gram = lax.psum(
        (gram_of(columns[:half], columns[:half]), gram_of(columns[half:], columns[half:])), "rows"
    )
    moving = jnp.concatenate(
        [columns[half:], right_factor[half:], moving_gram, moving_gram], axis=1
    )
    state = (columns[:half], right_factor[:half], moving, stay_gram)

    def advance(step_index, state):
        stay_cols, stay_fac, moving, stay_gram = state
        cross = gram_of(stay_cols, moving[:, :col_width])
        stay_cols, stay_fac, moving, stay_gram = one_step(
            stay_cols, stay_fac, moving, stay_gram, *summands(cross)
        )
        return stay_cols, stay_fac, lax.ppermute(moving, "blk", route), stay_gram

    stay_cols, stay_fac, moving, _ = lax.fori_loop(0, STEPS, advance, state)
    fac_end = col_width + right_factor.shape[1]
    return (
        jnp.concatenate([stay_cols, moving[:, :col_width]], axis=0),
        jnp.concatenate([stay_fac, moving[:, col_width:fac_end]], axis=0),
    )


def solution(mesh):
    return jax.shard_map(
        body,
        mesh=mesh,
        in_specs=(P("blk", "rows"), P("blk", "rows")),
        out_specs=(P("blk", "rows"), P("blk", "rows")),
        check_vma=False,
    )
```

time: 345 us -> 152 us (0.44)
  other arithmetic: 213 us -> 1.49 us
  Pallas kernels: 0 us -> 53 us
  blocking collectives: 57.1 us -> 10.4 us
  waiting for transfers between devices: 42.3 us -> 68.1 us
  matrix products: 23.3 us -> 4.5 us
  local copies, waits for them, and re-layouts: 4.8 us -> 13.3 us
    another operation x48 -> x0, other arithmetic: 212 us -> none  [the longest x18 74.8 us: rotation(): jnp.linalg.cholesky(jnp.dot(first.T, first, precision=HIGHEST_PREC))]
    pallas_call x0 -> x6, Pallas kernels: none -> 53 us  [one_step(): pl.pallas_call(step_kernel, out_shape=[jax.ShapeDtypeStruct(a.shape, a.dt...]
    psum x7 -> x1, blocking collectives: 57.1 us -> 10.4 us  [body(): lax.psum((gram_of(columns[:half], columns[:half]), gram_of(columns[half:]...]
    ppermute x18 -> x12, waiting for transfers between devices: 42.3 us -> 68.1 us  [the longest x6 52.2 us: advance(): return (stay_cols, stay_fac, lax.ppermute(moving, 'blk', route), stay_gram)]
    while x0 -> x54, local copies, waits for them, and re-layouts: none -> 13.2 us
    dot_general x44 -> x8, matrix products: 17.7 us -> 4.5 us  [dot_nt(): lax.dot_general(a, b, (((1,), (1,)), ((), ())), precision=HIGHEST_PREC, p...]
    another operation x6 -> x0, matrix products: 5.58 us -> none  [rotation(): return jax.scipy.linalg.solve_triangular(second, first.T, lower=True).T]
  transfers between devices with their start and end apart: 18 -> 12, of which waited for: 18 -> 12; matrix products, arithmetic and copies ran while one was open for 2% -> 5% of each run, Pallas kernels for 0% -> 0%
where the time goes in v2:
time: 152 us
  waiting for transfers between devices  68.1 us (45%)
  Pallas kernels  53 us (35%)
  local copies, waits for them, and re-layouts  13.3 us (9%)
  blocking collectives  10.4 us (7%)
  matrix products  4.5 us (3%)
    pallas_call x6, Pallas kernels, one_step(): pl.pallas_call(step_kernel, out_shape=[jax.ShapeDtypeStruct(a.shape, a.dt...  53 us
    ppermute x6, waiting for transfers between devices, advance(): return (stay_cols, stay_fac, lax.ppermute(moving, 'blk', route), stay_gram)  52.2 us
    ppermute x6, waiting for transfers between devices, summands(): return (part, lax.ppermute(part, 'rows', [(0, 1), (1, 0)]))  15.9 us
    while x54, local copies, waits for them, and re-layouts  13.2 us
    psum x1, blocking collectives, body(): lax.psum((gram_of(columns[:half], columns[:half]), gram_of(columns[half:]...  10.4 us
    dot_general x8, matrix products, dot_nt(): lax.dot_general(a, b, (((1,), (1,)), ((), ())), precision=HIGHEST_PREC, p...  4.5 us
  transfers between devices with their start and end apart: 12, of which 12 were waited for; matrix products, arithmetic and copies ran while one was open for 5% of the time, Pallas kernels for 0%

profile of v2, /device:TPU:0, one launch (start us, length us, event | category | flops | bytes accessed | tf_op | source)
XLA Modules:
  0.0 151.8 jit_solution(11350972758766758066)
XLA Ops:
  0.6 1.4 fusion.2
  2.0 1.3 fusion.4
  3.3 10.4 %all-reduce = (f32[64,64]{1,0:T(8,128)S(1)}, f32[64,64]{1,0:T(8,128)S(1)}) all-reduce(f32[64,64]{1,0:T(8,128)S(1)} %fusion.2, f32[64,64]{1,0:T(8,128)S(1)} %fusion.4), channel_id=1, replica_groups=mesh['blk'=16,'rows'=2] {'rows'}, use_global_device_ids=true, to_apply=%region_0.0 | all-reduce | flops 8192 | bytes 65536 | tf_op jit(solution)/shard_map/psum | solution.py:149
  13.9 136.4 %while.16 = (s32[]{:T(128)}, f32[64,640]{1,0:T(8,128)S(1)}, f32[64,256]{1,0:T(8,128)S(1)}, f32[64,1024]{1,0:T(8,128)S(1)}, f32[64,64]{1,0:T(8,128)S(1)}, /*index=5*/s32[]{:T(128)}) while((s32[]{:T(128)}, f32[64,640]{1,0:T(8,128)S(1)}, f32[64,256]{1,0:T(8,128)S(1)}, f32[64,1024]{1,0:T(8,128)S(1)}, f32[64,64]{1,0:T(8,128)S(1)}, ...), condition=%wide.region_3.0_spmd, body=%wide.region_2.0_spmd.sunk | while | flops 31457280 | bytes 2736361 | solution.py:165
  15.9 2.7 %collective-permute-done.peer_cross = f32[64,64]{1,0:T(8,128)S(1)} collective-permute-done((f32[64,64]{1,0:T(8,128)S(1)}, f32[64,64]{1,0:T(8,128)S(1)}, u32[]{:S(2)}, u32[]{:S(2)}) %collective-permute-start) | collective-permute-done | bytes 16416 | tf_op jit(solution)/shard_map/while/body/eval_jaxpr/ppermute | solution.py:136
  19.1 8.8 %turn.1 = (f32[64,640]{1,0:T(8,128)S(1)}, f32[64,256]{1,0:T(8,128)S(1)}, f32[64,1024]{1,0:T(8,128)}, f32[64,64]{1,0:T(8,128)S(1)}) custom-call(f32[64,640]{1,0:T(8,128)} %copy-done, f32[64,256]{1,0:T(8,128)} %copy.25.stay_fac, f32[64,1024]{1,0:T(8,128)S(1)} %get-tuple-element.102.moving, f32[64,64]{1,0:T(8,128)} %copy.26.stay_gram, f32[64,64]{1,0:T(8,128)} %copy-done.1, ...), custom_call_target="tpu_custom_call" | custom-call | tf_op jit(solution)/shard_map/while/body/eval_jaxpr/turn/pallas_call | solution.py:120
  28.0 8.7 %collective-permute-done.1 = f32[64,1024]{1,0:T(8,128)S(1)} collective-permute-done((f32[64,1024]{1,0:T(8,128)}, f32[64,1024]{1,0:T(8,128)S(1)}, u32[]{:S(2)}, u32[]{:S(2)}) %collective-permute-start.1) | collective-permute-done | bytes 262176 | tf_op jit(solution)/shard_map/while/body/eval_jaxpr/ppermute | solution.py:163
  38.6 2.7 %collective-permute-done.peer_cross = f32[64,64]{1,0:T(8,128)S(1)} collective-permute-done((f32[64,64]{1,0:T(8,128)S(1)}, f32[64,64]{1,0:T(8,128)S(1)}, u32[]{:S(2)}, u32[]{:S(2)}) %collective-permute-start) | collective-permute-done | bytes 16416 | tf_op jit(solution)/shard_map/while/body/eval_jaxpr/ppermute | solution.py:136
  41.9 8.8 %turn.1 = (f32[64,640]{1,0:T(8,128)S(1)}, f32[64,256]{1,0:T(8,128)S(1)}, f32[64,1024]{1,0:T(8,128)}, f32[64,64]{1,0:T(8,128)S(1)}) custom-call(f32[64,640]{1,0:T(8,128)} %copy-done, f32[64,256]{1,0:T(8,128)} %copy.25.stay_fac, f32[64,1024]{1,0:T(8,128)S(1)} %get-tuple-element.102.moving, f32[64,64]{1,0:T(8,128)} %copy.26.stay_gram, f32[64,64]{1,0:T(8,128)} %copy-done.1, ...), custom_call_target="tpu_custom_call" | custom-call | tf_op jit(solution)/shard_map/while/body/eval_jaxpr/turn/pallas_call | solution.py:120
  50.7 8.7 %collective-permute-done.1 = f32[64,1024]{1,0:T(8,128)S(1)} collective-permute-done((f32[64,1024]{1,0:T(8,128)}, f32[64,1024]{1,0:T(8,128)S(1)}, u32[]{:S(2)}, u32[]{:S(2)}) %collective-permute-start.1) | collective-permute-done | bytes 262176 | tf_op jit(solution)/shard_map/while/body/eval_jaxpr/ppermute | solution.py:163
  61.3 2.7 %collective-permute-done.peer_cross = f32[64,64]{1,0:T(8,128)S(1)} collective-permute-done((f32[64,64]{1,0:T(8,128)S(1)}, f32[64,64]{1,0:T(8,128)S(1)}, u32[]{:S(2)}, u32[]{:S(2)}) %collective-permute-start) | collective-permute-done | bytes 16416 | tf_op jit(solution)/shard_map/while/body/eval_jaxpr/ppermute | solution.py:136
  64.6 8.8 %turn.1 = (f32[64,640]{1,0:T(8,128)S(1)}, f32[64,256]{1,0:T(8,128)S(1)}, f32[64,1024]{1,0:T(8,128)}, f32[64,64]{1,0:T(8,128)S(1)}) custom-call(f32[64,640]{1,0:T(8,128)} %copy-done, f32[64,256]{1,0:T(8,128)} %copy.25.stay_fac, f32[64,1024]{1,0:T(8,128)S(1)} %get-tuple-element.102.moving, f32[64,64]{1,0:T(8,128)} %copy.26.stay_gram, f32[64,64]{1,0:T(8,128)} %copy-done.1, ...), custom_call_target="tpu_custom_call" | custom-call | tf_op jit(solution)/shard_map/while/body/eval_jaxpr/turn/pallas_call | solution.py:120
  73.4 8.7 %collective-permute-done.1 = f32[64,1024]{1,0:T(8,128)S(1)} collective-permute-done((f32[64,1024]{1,0:T(8,128)}, f32[64,1024]{1,0:T(8,128)S(1)}, u32[]{:S(2)}, u32[]{:S(2)}) %collective-permute-start.1) | collective-permute-done | bytes 262176 | tf_op jit(solution)/shard_map/while/body/eval_jaxpr/ppermute | solution.py:163
  84.1 2.7 %collective-permute-done.peer_cross = f32[64,64]{1,0:T(8,128)S(1)} collective-permute-done((f32[64,64]{1,0:T(8,128)S(1)}, f32[64,64]{1,0:T(8,128)S(1)}, u32[]{:S(2)}, u32[]{:S(2)}) %collective-permute-start) | collective-permute-done | bytes 16416 | tf_op jit(solution)/shard_map/while/body/eval_jaxpr/ppermute | solution.py:136
  87.3 8.8 %turn.1 = (f32[64,640]{1,0:T(8,128)S(1)}, f32[64,256]{1,0:T(8,128)S(1)}, f32[64,1024]{1,0:T(8,128)}, f32[64,64]{1,0:T(8,128)S(1)}) custom-call(f32[64,640]{1,0:T(8,128)} %copy-done, f32[64,256]{1,0:T(8,128)} %copy.25.stay_fac, f32[64,1024]{1,0:T(8,128)S(1)} %get-tuple-element.102.moving, f32[64,64]{1,0:T(8,128)} %copy.26.stay_gram, f32[64,64]{1,0:T(8,128)} %copy-done.1, ...), custom_call_target="tpu_custom_call" | custom-call | tf_op jit(solution)/shard_map/while/body/eval_jaxpr/turn/pallas_call | solution.py:120
  96.2 8.7 %collective-permute-done.1 = f32[64,1024]{1,0:T(8,128)S(1)} collective-permute-done((f32[64,1024]{1,0:T(8,128)}, f32[64,1024]{1,0:T(8,128)S(1)}, u32[]{:S(2)}, u32[]{:S(2)}) %collective-permute-start.1) | collective-permute-done | bytes 262176 | tf_op jit(solution)/shard_map/while/body/eval_jaxpr/ppermute | solution.py:163
  106.8 2.7 %collective-permute-done.peer_cross = f32[64,64]{1,0:T(8,128)S(1)} collective-permute-done((f32[64,64]{1,0:T(8,128)S(1)}, f32[64,64]{1,0:T(8,128)S(1)}, u32[]{:S(2)}, u32[]{:S(2)}) %collective-permute-start) | collective-permute-done | bytes 16416 | tf_op jit(solution)/shard_map/while/body/eval_jaxpr/ppermute | solution.py:136
  110.0 8.8 %turn.1 = (f32[64,640]{1,0:T(8,128)S(1)}, f32[64,256]{1,0:T(8,128)S(1)}, f32[64,1024]{1,0:T(8,128)}, f32[64,64]{1,0:T(8,128)S(1)}) custom-call(f32[64,640]{1,0:T(8,128)} %copy-done, f32[64,256]{1,0:T(8,128)} %copy.25.stay_fac, f32[64,1024]{1,0:T(8,128)S(1)} %get-tuple-element.102.moving, f32[64,64]{1,0:T(8,128)} %copy.26.stay_gram, f32[64,64]{1,0:T(8,128)} %copy-done.1, ...), custom_call_target="tpu_custom_call" | custom-call | tf_op jit(solution)/shard_map/while/body/eval_jaxpr/turn/pallas_call | solution.py:120
  118.9 8.7 %collective-permute-done.1 = f32[64,1024]{1,0:T(8,128)S(1)} collective-permute-done((f32[64,1024]{1,0:T(8,128)}, f32[64,1024]{1,0:T(8,128)S(1)}, u32[]{:S(2)}, u32[]{:S(2)}) %collective-permute-start.1) | collective-permute-done | bytes 262176 | tf_op jit(solution)/shard_map/while/body/eval_jaxpr/ppermute | solution.py:163
  129.5 2.7 %collective-permute-done.peer_cross = f32[64,64]{1,0:T(8,128)S(1)} collective-permute-done((f32[64,64]{1,0:T(8,128)S(1)}, f32[64,64]{1,0:T(8,128)S(1)}, u32[]{:S(2)}, u32[]{:S(2)}) %collective-permute-start) | collective-permute-done | bytes 16416 | tf_op jit(solution)/shard_map/while/body/eval_jaxpr/ppermute | solution.py:136
  132.8 8.8 %turn.1 = (f32[64,640]{1,0:T(8,128)S(1)}, f32[64,256]{1,0:T(8,128)S(1)}, f32[64,1024]{1,0:T(8,128)}, f32[64,64]{1,0:T(8,128)S(1)}) custom-call(f32[64,640]{1,0:T(8,128)} %copy-done, f32[64,256]{1,0:T(8,128)} %copy.25.stay_fac, f32[64,1024]{1,0:T(8,128)S(1)} %get-tuple-element.102.moving, f32[64,64]{1,0:T(8,128)} %copy.26.stay_gram, f32[64,64]{1,0:T(8,128)} %copy-done.1, ...), custom_call_target="tpu_custom_call" | custom-call | tf_op jit(solution)/shard_map/while/body/eval_jaxpr/turn/pallas_call | solution.py:120
  141.6 8.7 %collective-permute-done.1 = f32[64,1024]{1,0:T(8,128)S(1)} collective-permute-done((f32[64,1024]{1,0:T(8,128)}, f32[64,1024]{1,0:T(8,128)S(1)}, u32[]{:S(2)}, u32[]{:S(2)}) %collective-permute-start.1) | collective-permute-done | bytes 262176 | tf_op jit(solution)/shard_map/while/body/eval_jaxpr/ppermute | solution.py:163
  150.3 0.7 pad_maximum_fusion
  151.1 0.7 pad_maximum_fusion.2
  (81 shorter events, 15.2 us)
Async XLA Ops:
  0.6 13.2 %copy-start.2 = (f32[128,640]{1,0:T(8,128)S(1)}, f32[128,640]{1,0:T(8,128)}, u32[]{:S(2)}) copy-start(f32[128,640]{1,0:T(8,128)} %param.4) | copy-start | bytes 983044
  2.0 11.8 %copy-start.4 = (f32[128,256]{1,0:T(8,128)S(1)}, f32[128,256]{1,0:T(8,128)}, u32[]{:S(2)}) copy-start(f32[128,256]{1,0:T(8,128)} %param.5) | copy-start | bytes 393220
  14.0 0.7 copy-start
  14.6 0.6 copy-start.1
  14.6 3.9 %collective-permute-start = (f32[64,64]{1,0:T(8,128)S(1)}, f32[64,64]{1,0:T(8,128)S(1)}, u32[]{:S(2)}, u32[]{:S(2)}) collective-permute-start(f32[64,64]{1,0:T(8,128)S(1)} %fusion.14.cross), channel_id=1, source_target_pairs={{0,1},{1,0},{2,3},{3,2},{4,5},{5,4},{6,7},{7,6},{8,9},{9,8},{10,11... | collective-permute-start | bytes 49160 | tf_op jit(solution)/shard_map/while/body/eval_jaxpr/ppermute | solution.py:136
  28.0 8.7 %collective-permute-start.1 = (f32[64,1024]{1,0:T(8,128)}, f32[64,1024]{1,0:T(8,128)S(1)}, u32[]{:S(2)}, u32[]{:S(2)}) collective-permute-start(f32[64,1024]{1,0:T(8,128)} %get-tuple-element.91), channel_id=1, source_target_pairs={{30,0},{0,2},{2,4},{4,6},{6,8},{8,10},{10,12},{12,14},{14,16},{16,... | collective-permute-start | bytes 786440 | tf_op jit(solution)/shard_map/while/body/eval_jaxpr/ppermute | solution.py:163
  36.7 0.7 copy-start
  37.3 0.6 copy-start.1
  37.3 3.9 %collective-permute-start = (f32[64,64]{1,0:T(8,128)S(1)}, f32[64,64]{1,0:T(8,128)S(1)}, u32[]{:S(2)}, u32[]{:S(2)}) collective-permute-start(f32[64,64]{1,0:T(8,128)S(1)} %fusion.14.cross), channel_id=1, source_target_pairs={{0,1},{1,0},{2,3},{3,2},{4,5},{5,4},{6,7},{7,6},{8,9},{9,8},{10,11... | collective-permute-start | bytes 49160 | tf_op jit(solution)/shard_map/while/body/eval_jaxpr/ppermute | solution.py:136
  50.7 8.7 %collective-permute-start.1 = (f32[64,1024]{1,0:T(8,128)}, f32[64,1024]{1,0:T(8,128)S(1)}, u32[]{:S(2)}, u32[]{:S(2)}) collective-permute-start(f32[64,1024]{1,0:T(8,128)} %get-tuple-element.91), channel_id=1, source_target_pairs={{30,0},{0,2},{2,4},{4,6},{6,8},{8,10},{10,12},{12,14},{14,16},{16,... | collective-permute-start | bytes 786440 | tf_op jit(solution)/shard_map/while/body/eval_jaxpr/ppermute | solution.py:163
  59.4 0.7 copy-start
  60.1 0.6 copy-start.1
  60.1 3.9 %collective-permute-start = (f32[64,64]{1,0:T(8,128)S(1)}, f32[64,64]{1,0:T(8,128)S(1)}, u32[]{:S(2)}, u32[]{:S(2)}) collective-permute-start(f32[64,64]{1,0:T(8,128)S(1)} %fusion.14.cross), channel_id=1, source_target_pairs={{0,1},{1,0},{2,3},{3,2},{4,5},{5,4},{6,7},{7,6},{8,9},{9,8},{10,11... | collective-permute-start | bytes 49160 | tf_op jit(solution)/shard_map/while/body/eval_jaxpr/ppermute | solution.py:136
  73.4 8.7 %collective-permute-start.1 = (f32[64,1024]{1,0:T(8,128)}, f32[64,1024]{1,0:T(8,128)S(1)}, u32[]{:S(2)}, u32[]{:S(2)}) collective-permute-start(f32[64,1024]{1,0:T(8,128)} %get-tuple-element.91), channel_id=1, source_target_pairs={{30,0},{0,2},{2,4},{4,6},{6,8},{8,10},{10,12},{12,14},{14,16},{16,... | collective-permute-start | bytes 786440 | tf_op jit(solution)/shard_map/while/body/eval_jaxpr/ppermute | solution.py:163
  82.1 0.7 copy-start
  82.8 0.6 copy-start.1
  82.8 3.9 %collective-permute-start = (f32[64,64]{1,0:T(8,128)S(1)}, f32[64,64]{1,0:T(8,128)S(1)}, u32[]{:S(2)}, u32[]{:S(2)}) collective-permute-start(f32[64,64]{1,0:T(8,128)S(1)} %fusion.14.cross), channel_id=1, source_target_pairs={{0,1},{1,0},{2,3},{3,2},{4,5},{5,4},{6,7},{7,6},{8,9},{9,8},{10,11... | collective-permute-start | bytes 49160 | tf_op jit(solution)/shard_map/while/body/eval_jaxpr/ppermute | solution.py:136
  96.2 8.7 %collective-permute-start.1 = (f32[64,1024]{1,0:T(8,128)}, f32[64,1024]{1,0:T(8,128)S(1)}, u32[]{:S(2)}, u32[]{:S(2)}) collective-permute-start(f32[64,1024]{1,0:T(8,128)} %get-tuple-element.91), channel_id=1, source_target_pairs={{30,0},{0,2},{2,4},{4,6},{6,8},{8,10},{10,12},{12,14},{14,16},{16,... | collective-permute-start | bytes 786440 | tf_op jit(solution)/shard_map/while/body/eval_jaxpr/ppermute | solution.py:163
  104.9 0.7 copy-start
  105.5 3.9 %collective-permute-start = (f32[64,64]{1,0:T(8,128)S(1)}, f32[64,64]{1,0:T(8,128)S(1)}, u32[]{:S(2)}, u32[]{:S(2)}) collective-permute-start(f32[64,64]{1,0:T(8,128)S(1)} %fusion.14.cross), channel_id=1, source_target_pairs={{0,1},{1,0},{2,3},{3,2},{4,5},{5,4},{6,7},{7,6},{8,9},{9,8},{10,11... | collective-permute-start | bytes 49160 | tf_op jit(solution)/shard_map/while/body/eval_jaxpr/ppermute | solution.py:136
  118.9 8.7 %collective-permute-start.1 = (f32[64,1024]{1,0:T(8,128)}, f32[64,1024]{1,0:T(8,128)S(1)}, u32[]{:S(2)}, u32[]{:S(2)}) collective-permute-start(f32[64,1024]{1,0:T(8,128)} %get-tuple-element.91), channel_id=1, source_target_pairs={{30,0},{0,2},{2,4},{4,6},{6,8},{8,10},{10,12},{12,14},{14,16},{16,... | collective-permute-start | bytes 786440 | tf_op jit(solution)/shard_map/while/body/eval_jaxpr/ppermute | solution.py:163
  127.6 0.7 copy-start
  128.3 3.9 %collective-permute-start = (f32[64,64]{1,0:T(8,128)S(1)}, f32[64,64]{1,0:T(8,128)S(1)}, u32[]{:S(2)}, u32[]{:S(2)}) collective-permute-start(f32[64,64]{1,0:T(8,128)S(1)} %fusion.14.cross), channel_id=1, source_target_pairs={{0,1},{1,0},{2,3},{3,2},{4,5},{5,4},{6,7},{7,6},{8,9},{9,8},{10,11... | collective-permute-start | bytes 49160 | tf_op jit(solution)/shard_map/while/body/eval_jaxpr/ppermute | solution.py:136
  141.6 8.7 %collective-permute-start.1 = (f32[64,1024]{1,0:T(8,128)}, f32[64,1024]{1,0:T(8,128)S(1)}, u32[]{:S(2)}, u32[]{:S(2)}) collective-permute-start(f32[64,1024]{1,0:T(8,128)} %get-tuple-element.91), channel_id=1, source_target_pairs={{30,0},{0,2},{2,4},{4,6},{6,8},{8,10},{10,12},{12,14},{14,16},{16,... | collective-permute-start | bytes 786440 | tf_op jit(solution)/shard_map/while/body/eval_jaxpr/ppermute | solution.py:163
  (8 other events, 4.9 us)

commit v3 on v2

v3 whole, which is shorter than its diff:
```python
import jax
import jax.numpy as jnp
from jax import lax
from jax.experimental import pallas as pl
from jax.experimental.pallas import tpu as pltpu
from jax.sharding import PartitionSpec as P

STEPS = 6
PANEL = 16
LANES = 128
MESH = pl.DeviceIdType.MESH

HIGHEST_PREC = lax.Precision.HIGHEST


def dot_nn(a, b):
    return lax.dot_general(
        a, b, (((1,), (0,)), ((), ())), precision=HIGHEST_PREC, preferred_element_type=jnp.float32
    )


def dot_nt(a, b):
    return lax.dot_general(
        a, b, (((1,), (1,)), ((), ())), precision=HIGHEST_PREC, preferred_element_type=jnp.float32
    )


def dot_tn(a, b):
    return lax.dot_general(
        a, b, (((0,), (0,)), ((), ())), precision=HIGHEST_PREC, preferred_element_type=jnp.float32
    )


def eliminate(work):
    order, width = work.shape
    panels = order // PANEL
    for panel in range(panels):
        low = panel * PANEL
        high = low + PANEL
        end = min(high + PANEL, order)
        rows = work[low:high, :]
        below = work[high:end, :] if end > high else None
        spread = [
            jnp.broadcast_to(rows[:, low + k : low + k + 1], (PANEL, 128)) for k in range(PANEL)
        ]
        spread_below = None
        if below is not None:
            spread_below = [
                jnp.broadcast_to(below[:, low + k : low + k + 1], (end - high, 128))
                for k in range(PANEL)
            ]
        done = []
        for j in range(PANEL):
            scale = lax.rsqrt(spread[j][j : j + 1, :])
            column = spread[j] * scale
            wide = jnp.concatenate([scale] * (width // 128), axis=1)
            pivot_row = rows[j : j + 1, :] * wide
            done.append(pivot_row)
            wide_column = jnp.concatenate([column] * (width // 128), axis=1)
            if j + 1 < PANEL:
                rows = rows - wide_column * pivot_row
            if below is not None:
                column_below = spread_below[j] * scale
                wide_below = jnp.concatenate([column_below] * (width // 128), axis=1)
                below = below - wide_below * pivot_row
            for k in range(j + 1, PANEL):
                head = spread[k][j : j + 1, :] * scale
                spread[k] = spread[k] - column * head
                if below is not None:
                    spread_below[k] = spread_below[k] - column_below * head
        finished = jnp.concatenate(done, axis=0)
        work[low:high, :] = finished
        if below is not None:
            work[high:end, :] = below
        if end < order:
            work[end:, :] = work[end:, :] - dot_tn(finished[:, end:order], finished)


def lanes(chunk):
    return slice(chunk * LANES, (chunk + 1) * LANES)


def cycle_kernel(
    columns, right_factor, new_columns, new_factor, stay, sent, held, grams, stay_gram, gram, work,
    solve, sent_sem, held_sem, gram_sent_sem, gram_sem,
):
    half = columns.shape[0] // 2
    order = 2 * half
    col_chunks = columns.shape[1] // LANES
    chunks = col_chunks + right_factor.shape[1] // LANES
    ring, peers = lax.axis_size("blk"), lax.axis_size("rows")
    place, row_place = lax.axis_index("blk"), lax.axis_index("rows")
    right, left = lax.rem(place + 1, ring), lax.rem(place + ring - 1, ring)

    barrier = pltpu.get_barrier_semaphore()
    for neighbour in (left, right):
        pl.semaphore_signal(barrier, inc=1, device_id={"blk": neighbour}, device_id_type=MESH)
    for off in range(1, peers):
        peer = lax.rem(row_place + off, peers)
        pl.semaphore_signal(barrier, inc=1, device_id={"rows": peer}, device_id_type=MESH)

    def gram_copy(step, off, first):
        part = grams.at[step, row_place]
        if not first:
            part = part.at[pl.ds(half, half)]
        return pltpu.make_async_remote_copy(
            src_ref=part,
            dst_ref=part,
            send_sem=gram_sent_sem.at[step, off - 1],
            recv_sem=gram_sem.at[step, off - 1],
            device_id={"rows": lax.rem(row_place + off, peers)},
            device_id_type=MESH,
        )

    def ring_copy(step, chunk):
        return pltpu.make_async_remote_copy(
            src_ref=sent.at[step, chunk],
            dst_ref=held.at[step + 1, chunk],
            send_sem=sent_sem.at[step, chunk],
            recv_sem=held_sem.at[step, chunk],
            device_id={"blk": right},
            device_id_type=MESH,
        )

    total = jnp.zeros((order, order), jnp.float32)
    for chunk in range(chunks):
        source = columns if chunk < col_chunks else right_factor
        at = lanes(chunk if chunk < col_chunks else chunk - col_chunks)
        stay[chunk] = source[:half, at]
        held[0, chunk] = source[half:, at]
        if chunk < col_chunks:
            total = total + dot_nt(source[:, at], source[:, at])
    grams[0, row_place] = total
    pl.semaphore_wait(barrier, 2 + peers - 1)
    for off in range(1, peers):
        gram_copy(0, off, True).start()
    for off in range(1, peers):
        gram_copy(0, off, True).wait()
    first_gram = grams[0, 0, :half, :half]
    for peer in range(1, peers):
        first_gram = first_gram + grams[0, peer, :half, :half]
    stay_gram[...] = first_gram

    def advance(step, carry):
        @pl.when(step > 0)
        def _():
            for off in range(1, peers):
                gram_copy(step, off, False).wait()

        lower = grams[step, 0, half:, :]
        for peer in range(1, peers):
            lower = lower + grams[step, peer, half:, :]
        gram[:half, :half] = stay_gram[...]
        gram[:half, half:] = lower[:, :half].T
        gram[half:, :] = lower
        g = gram[...]
        work[...] = dot_nn(g, g)
        eliminate(work)
        upper = work[...]
        keep = lax.broadcasted_iota(jnp.int32, upper.shape, 0) <= lax.broadcasted_iota(
            jnp.int32, upper.shape, 1
        )
        upper = jnp.where(keep, upper, 0.0)
        solve[:, :order] = dot_nt(upper, upper)
        solve[:, order:] = upper
        eliminate(solve)
        turn = solve[:, order:]
        top, low = turn[:half], turn[half:]

        def pair(chunk):
            return jnp.concatenate([stay[chunk], held[step, chunk]], axis=0)

        for chunk in range(col_chunks):
            sent[step, chunk] = dot_nn(low, pair(chunk))
            ring_copy(step, chunk).start()

        @pl.when(step > 0)
        def _():
            for chunk in range(col_chunks, chunks):
                ring_copy(step - 1, chunk).wait_recv()

        for chunk in range(col_chunks, chunks):
            sent[step, chunk] = dot_nn(low, pair(chunk))
            ring_copy(step, chunk).start()
        for chunk in range(chunks):
            stay[chunk] = dot_nn(top, pair(chunk))
        stay_gram[...] = dot_nt(dot_nn(top, g), top)

        @pl.when(step < STEPS - 1)
        def _():
            total = jnp.zeros((half, order), jnp.float32)
            for chunk in range(col_chunks):
                ring_copy(step, chunk).wait_recv()
                moving = held[step + 1, chunk]
                total = total + dot_nt(moving, jnp.concatenate([stay[chunk], moving], axis=0))
            grams[step + 1, row_place, half:, :] = total
            for off in range(1, peers):
                gram_copy(step + 1, off, False).start()

        for chunk in range(chunks):
            ring_copy(step, chunk).wait_send()
        return carry

    lax.fori_loop(0, STEPS, advance, 0)
    for chunk in range(chunks):
        ring_copy(STEPS - 1, chunk).wait_recv()
        target = new_columns if chunk < col_chunks else new_factor
        at = lanes(chunk if chunk < col_chunks else chunk - col_chunks)
        target[:half, at] = stay[chunk]
        target[half:, at] = held[STEPS, chunk]


def body(columns, right_factor):
    order = columns.shape[0]
    half = order // 2
    chunks = (columns.shape[1] + right_factor.shape[1]) // LANES
    peers = lax.axis_size("rows")
    return pl.pallas_call(
        cycle_kernel,
        out_shape=[jax.ShapeDtypeStruct(a.shape, a.dtype) for a in (columns, right_factor)],
        in_specs=[pl.BlockSpec(memory_space=pltpu.VMEM)] * 2,
        out_specs=[pl.BlockSpec(memory_space=pltpu.VMEM)] * 2,
        scratch_shapes=[
            pltpu.VMEM((chunks, half, LANES), jnp.float32),
            pltpu.VMEM((STEPS, chunks, half, LANES), jnp.float32),
            pltpu.VMEM((STEPS + 1, chunks, half, LANES), jnp.float32),
            pltpu.VMEM((STEPS, peers, order, order), jnp.float32),
            pltpu.VMEM((half, half), jnp.float32),
            pltpu.VMEM((order, order), jnp.float32),
            pltpu.VMEM((order, order), jnp.float32),
            pltpu.VMEM((order, 2 * order), jnp.float32),
            pltpu.SemaphoreType.DMA((STEPS, chunks)),
            pltpu.SemaphoreType.DMA((STEPS, chunks)),
            pltpu.SemaphoreType.DMA((STEPS, peers - 1)),
            pltpu.SemaphoreType.DMA((STEPS, peers - 1)),
        ],
        compiler_params=pltpu.CompilerParams(collective_id=0, has_side_effects=True),
        name="cycle",
    )(columns, right_factor)


def solution(mesh):
    return jax.shard_map(
        body,
        mesh=mesh,
        in_specs=(P("blk", "rows"), P("blk", "rows")),
        out_specs=(P("blk", "rows"), P("blk", "rows")),
        check_vma=False,
    )
```

time: 152 us -> 88.7 us (0.58)
  waiting for transfers between devices: 68.1 us -> 0 us
  Pallas kernels: 53 us -> 85.5 us
  local copies, waits for them, and re-layouts: 13.3 us -> 2.41 us
  blocking collectives: 10.4 us -> 0 us
  matrix products: 4.5 us -> 0 us
    ppermute x12 -> x0, waiting for transfers between devices: 68.1 us -> none  [the longest x6 52.2 us: advance(): return (stay_cols, stay_fac, lax.ppermute(moving, 'blk', route), stay_gram)]
    pallas_call x6 -> x1, Pallas kernels: 53 us -> 85.5 us  [body(): pl.pallas_call(cycle_kernel, out_shape=[jax.ShapeDtypeStruct(a.shape, a.d...]
    while x54 -> x0, local copies, waits for them, and re-layouts: 13.2 us -> none
    psum x1 -> x0, blocking collectives: 10.4 us -> none  [body(): lax.psum((gram_of(columns[:half], columns[:half]), gram_of(columns[half:]...]
    dot_general x8 -> x0, matrix products: 4.5 us -> none  [dot_nt(): lax.dot_general(a, b, (((1,), (1,)), ((), ())), precision=HIGHEST_PREC, p...]
    unnamed x4, local copies, waits for them, and re-layouts: 0.01 us -> 2.41 us
  transfers between devices with their start and end apart: 12 -> 0, of which waited for: 12 -> 0; matrix products, arithmetic and copies ran while one was open for 5% -> 0% of each run, Pallas kernels for 0% -> 0%
where the time goes in v3:
time: 88.7 us; the launch traced here: 88.6 us
  Pallas kernels  85.5 us (96%)
  local copies, waits for them, and re-layouts  2.41 us (3%)
    pallas_call x1, Pallas kernels, body(): pl.pallas_call(cycle_kernel, out_shape=[jax.ShapeDtypeStruct(a.shape, a.d...  85.5 us
    unnamed x4, local copies, waits for them, and re-layouts  2.41 us

profile of v3, /device:TPU:0, one launch (start us, length us, event | category | flops | bytes accessed | tf_op | source)
XLA Modules:
  0.0 88.6 jit_solution(10144136175171193631)
XLA Ops:
  0.6 85.5 %cycle.1 = (f32[128,640]{1,0:T(8,128)}, f32[128,256]{1,0:T(8,128)}) custom-call(f32[128,640]{1,0:T(8,128)} %columns.1, f32[128,256]{1,0:T(8,128)} %right_factor.1), custom_call_target="tpu_custom_call" | custom-call | tf_op jit(solution)/shard_map/cycle/pallas_call | solution.py:218
  86.2 0.0 copy-start
  86.2 1.8 %copy.6 = f32[128,640]{1,0:T(8,128)} copy(f32[128,640]{1,0:T(8,128)} %get-tuple-element.4) | data formatting | bytes 655360
  87.9 0.0 copy-done
  87.9 0.7 copy.7
Async XLA Ops:
  86.2 1.8 %copy-start = (f32[128,256]{1,0:T(8,128)S(1)}, f32[128,256]{1,0:T(8,128)}, u32[]{:S(2)}) copy-start(f32[128,256]{1,0:T(8,128)} %get-tuple-element.5) | copy-start | bytes 393220

commit v4 on v3

v4 whole, which is shorter than its diff:
```python
import jax
import jax.numpy as jnp
from jax import lax
from jax.experimental import pallas as pl
from jax.experimental.pallas import tpu as pltpu
from jax.sharding import PartitionSpec as P

STEPS = 6
PANEL = 16
LANES = 128
MESH = pl.DeviceIdType.MESH

HIGHEST_PREC = lax.Precision.HIGHEST


def dot_nn(a, b):
    return lax.dot_general(
        a, b, (((1,), (0,)), ((), ())), precision=HIGHEST_PREC, preferred_element_type=jnp.float32
    )


def dot_nt(a, b):
    return lax.dot_general(
        a, b, (((1,), (1,)), ((), ())), precision=HIGHEST_PREC, preferred_element_type=jnp.float32
    )


def dot_tn(a, b):
    return lax.dot_general(
        a, b, (((0,), (0,)), ((), ())), precision=HIGHEST_PREC, preferred_element_type=jnp.float32
    )


def eliminate(work, midway=None):
    order, width = work.shape
    panels = order // PANEL
    for panel in range(panels):
        if midway is not None and panel == panels // 2 - 1:
            midway()
        low = panel * PANEL
        high = low + PANEL
        end = min(high + PANEL, order)
        rows = work[low:high, :]
        below = work[high:end, :] if end > high else None
        spread = [
            jnp.broadcast_to(rows[:, low + k : low + k + 1], (PANEL, 128)) for k in range(PANEL)
        ]
        spread_below = None
        if below is not None:
            spread_below = [
                jnp.broadcast_to(below[:, low + k : low + k + 1], (end - high, 128))
                for k in range(PANEL)
            ]
        done = []
        for j in range(PANEL):
            scale = lax.rsqrt(spread[j][j : j + 1, :])
            column = spread[j] * scale
            wide = jnp.concatenate([scale] * (width // 128), axis=1)
            pivot_row = rows[j : j + 1, :] * wide
            done.append(pivot_row)
            wide_column = jnp.concatenate([column] * (width // 128), axis=1)
            if j + 1 < PANEL:
                rows = rows - wide_column * pivot_row
            if below is not None:
                column_below = spread_below[j] * scale
                wide_below = jnp.concatenate([column_below] * (width // 128), axis=1)
                below = below - wide_below * pivot_row
            for k in range(j + 1, PANEL):
                head = spread[k][j : j + 1, :] * scale
                spread[k] = spread[k] - column * head
                if below is not None:
                    spread_below[k] = spread_below[k] - column_below * head
        finished = jnp.concatenate(done, axis=0)
        work[low:high, :] = finished
        if below is not None:
            work[high:end, :] = below
        if end < order:
            work[end:, :] = work[end:, :] - dot_tn(finished[:, end:order], finished)


def lanes(chunk):
    return slice(chunk * LANES, (chunk + 1) * LANES)


def cycle_kernel(
    columns, right_factor, new_columns, new_factor, own, near, stay_fac, sent_fac, held_fac, grams,
    near_grams, lows, near_lows, cross, work, solve, pair_sent, pair_sem, fac_sent, fac_sem, gram_sent,
    gram_sem, low_sent, low_sem, cross_sent, cross_sem,
):
    half = columns.shape[0] // 2
    order = 2 * half
    col_chunks = columns.shape[1] // LANES
    fac_chunks = right_factor.shape[1] // LANES
    ring, peers = lax.axis_size("blk"), lax.axis_size("rows")
    place, row_place = lax.axis_index("blk"), lax.axis_index("rows")
    right, left = lax.rem(place + 1, ring), lax.rem(place + ring - 1, ring)

    barrier = pltpu.get_barrier_semaphore()
    for neighbour in (left, right):
        pl.semaphore_signal(barrier, inc=1, device_id={"blk": neighbour}, device_id_type=MESH)
    for off in range(1, peers):
        peer = lax.rem(row_place + off, peers)
        pl.semaphore_signal(barrier, inc=1, device_id={"rows": peer}, device_id_type=MESH)

    def to_right(source, target, send_sem, recv_sem):
        return pltpu.make_async_remote_copy(
            src_ref=source,
            dst_ref=target,
            send_sem=send_sem,
            recv_sem=recv_sem,
            device_id={"blk": right},
            device_id_type=MESH,
        )

    def pair_copy(step, chunk):
        return to_right(
            own.at[step, chunk], near.at[step, chunk], pair_sent.at[step, chunk], pair_sem.at[step, chunk]
        )

    def fac_copy(step, chunk):
        return to_right(
            sent_fac.at[step, chunk],
            held_fac.at[step + 1, chunk],
            fac_sent.at[step, chunk],
            fac_sem.at[step, chunk],
        )

    def gram_copy(step):
        return to_right(grams.at[step], near_grams.at[step], gram_sent.at[step], gram_sem.at[step])

    def low_copy(step):
        return to_right(lows.at[step], near_lows.at[step], low_sent.at[step], low_sem.at[step])

    def cross_copy(slot, off):
        part = cross.at[slot, row_place]
        return pltpu.make_async_remote_copy(
            src_ref=part,
            dst_ref=part,
            send_sem=cross_sent.at[slot, off - 1],
            recv_sem=cross_sem.at[slot, off - 1],
            device_id={"rows": lax.rem(row_place + off, peers)},
            device_id_type=MESH,
        )

    def cross_sum(slot):
        total = cross[slot, 0]
        for peer in range(1, peers):
            total = total + cross[slot, peer]
        return total

    total = jnp.zeros((order, order), jnp.float32)
    for chunk in range(col_chunks):
        part = columns[:, lanes(chunk)]
        own[0, chunk] = part
        total = total + dot_nt(part, part)
    cross[0, row_place] = total
    for chunk in range(fac_chunks):
        stay_fac[chunk] = right_factor[:half, lanes(chunk)]
        held_fac[0, chunk] = right_factor[half:, lanes(chunk)]
    pl.semaphore_wait(barrier, 2 + peers - 1)
    for off in range(1, peers):
        cross_copy(0, off).start()
    for chunk in range(col_chunks):
        pair_copy(0, chunk).start()
    for off in range(1, peers):
        cross_copy(0, off).wait()
    grams[0] = cross_sum(0)

    def advance(step, carry):
        gram_copy(step).start()
        g = grams[step]
        work[...] = dot_nn(g, g)
        eliminate(work)
        upper = work[...]
        keep = lax.broadcasted_iota(jnp.int32, upper.shape, 0) <= lax.broadcasted_iota(
            jnp.int32, upper.shape, 1
        )
        upper = jnp.where(keep, upper, 0.0)
        solve[:, :order] = dot_nt(upper, upper)
        solve[:, order:] = upper

        def products():
            for chunk in range(col_chunks):
                pair_copy(step, chunk).wait_recv()

            @pl.when(step < STEPS - 1)
            def _():
                total = jnp.zeros((order, order), jnp.float32)
                for chunk in range(col_chunks):
                    total = total + dot_nt(own[step, chunk], near[step, chunk])
                cross[step + 1, row_place] = total
                for off in range(1, peers):
                    cross_copy(step + 1, off).start()

        eliminate(solve, products)
        turn = solve[:, order:]
        top, low = turn[:half], turn[half:]
        lows[step] = low
        low_copy(step).start()

        for chunk in range(col_chunks):
            own[step + 1, chunk, :half] = dot_nn(top, own[step, chunk])

        @pl.when(step > 0)
        def _():
            for chunk in range(fac_chunks):
                fac_copy(step - 1, chunk).wait_recv()

        for chunk in range(fac_chunks):
            turned = dot_nn(turn, jnp.concatenate([stay_fac[chunk], held_fac[step, chunk]], axis=0))
            stay_fac[chunk] = turned[:half]
            sent_fac[step, chunk] = turned[half:]
            fac_copy(step, chunk).start()
        gram_copy(step).wait_recv()

        @pl.when(step < STEPS - 1)
        def _():
            grams[step + 1, :half, :half] = dot_nt(dot_nn(top, grams[step]), top)
            for off in range(1, peers):
                cross_copy(step + 1, off).wait()
            reach = dot_nn(top, cross_sum(step + 1))
            low_copy(step).wait_recv()
            arrived = near_lows[step]
            term = dot_nt(reach, arrived)
            grams[step + 1, :half, half:] = term
            grams[step + 1, half:, :half] = term.T
            grams[step + 1, half:, half:] = dot_nt(dot_nn(arrived, near_grams[step]), arrived)
            for chunk in range(col_chunks):
                own[step + 1, chunk, half:] = dot_nn(arrived, near[step, chunk])
                pair_copy(step + 1, chunk).start()

        for chunk in range(col_chunks):
            pair_copy(step, chunk).wait_send()
        for chunk in range(fac_chunks):
            fac_copy(step, chunk).wait_send()
        gram_copy(step).wait_send()
        low_copy(step).wait_send()
        return carry

    lax.fori_loop(0, STEPS, advance, 0)
    low_copy(STEPS - 1).wait_recv()
    for chunk in range(col_chunks):
        new_columns[:half, lanes(chunk)] = own[STEPS, chunk, :half]
        new_columns[half:, lanes(chunk)] = dot_nn(near_lows[STEPS - 1], near[STEPS - 1, chunk])
    for chunk in range(fac_chunks):
        fac_copy(STEPS - 1, chunk).wait_recv()
        new_factor[:half, lanes(chunk)] = stay_fac[chunk]
        new_factor[half:, lanes(chunk)] = held_fac[STEPS, chunk]


def body(columns, right_factor):
    order = columns.shape[0]
    half = order // 2
    col_chunks = columns.shape[1] // LANES
    fac_chunks = right_factor.shape[1] // LANES
    peers = lax.axis_size("rows")

    def room(*shape):
        return pltpu.VMEM(shape, jnp.float32)

    return pl.pallas_call(
        cycle_kernel,
        out_shape=[jax.ShapeDtypeStruct(a.shape, a.dtype) for a in (columns, right_factor)],
        in_specs=[pl.BlockSpec(memory_space=pltpu.VMEM)] * 2,
        out_specs=[pl.BlockSpec(memory_space=pltpu.VMEM)] * 2,
        scratch_shapes=[
            room(STEPS + 1, col_chunks, order, LANES),
            room(STEPS, col_chunks, order, LANES),
            room(fac_chunks, half, LANES),
            room(STEPS, fac_chunks, half, LANES),
            room(STEPS + 1, fac_chunks, half, LANES),
            room(STEPS, order, order),
            room(STEPS, order, order),
            room(STEPS, half, order),
            room(STEPS, half, order),
            room(STEPS, peers, order, order),
            room(order, order),
            room(order, 2 * order),
            pltpu.SemaphoreType.DMA((STEPS, col_chunks)),
            pltpu.SemaphoreType.DMA((STEPS, col_chunks)),
            pltpu.SemaphoreType.DMA((STEPS, fac_chunks)),
            pltpu.SemaphoreType.DMA((STEPS, fac_chunks)),
            pltpu.SemaphoreType.DMA((STEPS,)),
            pltpu.SemaphoreType.DMA((STEPS,)),
            pltpu.SemaphoreType.DMA((STEPS,)),
            pltpu.SemaphoreType.DMA((STEPS,)),
            pltpu.SemaphoreType.DMA((STEPS, peers - 1)),
            pltpu.SemaphoreType.DMA((STEPS, peers - 1)),
        ],
        compiler_params=pltpu.CompilerParams(collective_id=0, has_side_effects=True),
        name="cycle",
    )(columns, right_factor)


def solution(mesh):
    return jax.shard_map(
        body,
        mesh=mesh,
        in_specs=(P("blk", "rows"), P("blk", "rows")),
        out_specs=(P("blk", "rows"), P("blk", "rows")),
        check_vma=False,
    )
```

time: 88.7 us -> 77.3 us (0.87)
  Pallas kernels: 85.5 us -> 74.1 us
    pallas_call x1, Pallas kernels: 85.5 us -> 74.1 us  [body(): pl.pallas_call(cycle_kernel, out_shape=[jax.ShapeDtypeStruct(a.shape, a.d...]
where the time goes in v4:
time: 77.3 us; the launch traced here: 77.2 us
  Pallas kernels  74.1 us (96%)
  local copies, waits for them, and re-layouts  2.41 us (3%)
    pallas_call x1, Pallas kernels, body(): pl.pallas_call(cycle_kernel, out_shape=[jax.ShapeDtypeStruct(a.shape, a.d...  74.1 us
    unnamed x4, local copies, waits for them, and re-layouts  2.41 us

profile of v4, /device:TPU:0, one launch (start us, length us, event | category | flops | bytes accessed | tf_op | source)
XLA Modules:
  0.0 77.2 jit_solution(5254872585689441689)
XLA Ops:
  0.6 74.1 %cycle.1 = (f32[128,640]{1,0:T(8,128)}, f32[128,256]{1,0:T(8,128)}) custom-call(f32[128,640]{1,0:T(8,128)} %columns.1, f32[128,256]{1,0:T(8,128)} %right_factor.1), custom_call_target="tpu_custom_call" | custom-call | tf_op jit(solution)/shard_map/cycle/pallas_call | solution.py:261
  74.7 0.0 copy-start
  74.7 1.8 %copy.6 = f32[128,640]{1,0:T(8,128)} copy(f32[128,640]{1,0:T(8,128)} %get-tuple-element.4) | data formatting | bytes 655360
  76.5 0.0 copy-done
  76.5 0.7 copy.7
Async XLA Ops:
  74.7 1.8 %copy-start = (f32[128,256]{1,0:T(8,128)S(1)}, f32[128,256]{1,0:T(8,128)}, u32[]{:S(2)}) copy-start(f32[128,256]{1,0:T(8,128)} %get-tuple-element.5) | copy-start | bytes 393220

commit v5 on v4

--- a/solution.py
+++ b/solution.py
@@ -221,20 +221,13 @@
             reach = dot_nn(top, cross_sum(step + 1))
             low_copy(step).wait_recv()
             arrived = near_lows[step]
-            term = dot_nt(reach, arrived)
-            grams[step + 1, :half, half:] = term
-            grams[step + 1, half:, :half] = term.T
+            grams[step + 1, :half, half:] = dot_nt(reach, arrived)
+            grams[step + 1, half:, :half] = dot_nt(arrived, reach)
             grams[step + 1, half:, half:] = dot_nt(dot_nn(arrived, near_grams[step]), arrived)
             for chunk in range(col_chunks):
                 own[step + 1, chunk, half:] = dot_nn(arrived, near[step, chunk])
                 pair_copy(step + 1, chunk).start()
 
-        for chunk in range(col_chunks):
-            pair_copy(step, chunk).wait_send()
-        for chunk in range(fac_chunks):
-            fac_copy(step, chunk).wait_send()
-        gram_copy(step).wait_send()
-        low_copy(step).wait_send()
         return carry
 
     lax.fori_loop(0, STEPS, advance, 0)
@@ -246,6 +239,17 @@
         fac_copy(STEPS - 1, chunk).wait_recv()
         new_factor[:half, lanes(chunk)] = stay_fac[chunk]
         new_factor[half:, lanes(chunk)] = held_fac[STEPS, chunk]
+
+    def settle(step, carry):
+        for chunk in range(col_chunks):
+            pair_copy(step, chunk).wait_send()
+        for chunk in range(fac_chunks):
+            fac_copy(step, chunk).wait_send()
+        gram_copy(step).wait_send()
+        low_copy(step).wait_send()
+        return carry
+
+    lax.fori_loop(0, STEPS, settle, 0)
 
 
 def body(columns, right_factor):

time: 77.3 us -> 77.7 us (level)
  no operation moved by 1% of the time
where the time goes in v5:
time: 77.7 us; the launch traced here: 77.5 us
  Pallas kernels  74.4 us (96%)
  local copies, waits for them, and re-layouts  2.41 us (3%)
    pallas_call x1, Pallas kernels, body(): pl.pallas_call(cycle_kernel, out_shape=[jax.ShapeDtypeStruct(a.shape, a.d...  74.4 us
    unnamed x4, local copies, waits for them, and re-layouts  2.41 us

profile of v5, /device:TPU:0, one launch (start us, length us, event | category | flops | bytes accessed | tf_op | source)
XLA Modules:
  0.0 77.5 jit_solution(15786694325122810830)
XLA Ops:
  0.6 74.4 %cycle.1 = (f32[128,640]{1,0:T(8,128)}, f32[128,256]{1,0:T(8,128)}) custom-call(f32[128,640]{1,0:T(8,128)} %columns.1, f32[128,256]{1,0:T(8,128)} %right_factor.1), custom_call_target="tpu_custom_call" | custom-call | tf_op jit(solution)/shard_map/cycle/pallas_call | solution.py:265
  75.1 0.0 copy-start
  75.1 1.8 %copy.6 = f32[128,640]{1,0:T(8,128)} copy(f32[128,640]{1,0:T(8,128)} %get-tuple-element.4) | data formatting | bytes 655360
  76.8 0.0 copy-done
  76.8 0.7 copy.7
Async XLA Ops:
  75.1 1.8 %copy-start = (f32[128,256]{1,0:T(8,128)S(1)}, f32[128,256]{1,0:T(8,128)}, u32[]{:S(2)}) copy-start(f32[128,256]{1,0:T(8,128)} %get-tuple-element.5) | copy-start | bytes 393220
